TPU v7x, 256 devices: a whole 4x4x8 slice. The times are simulated.
256 devices in a mesh: row: 8 (over y, core), col: 32 (over x, z).
Axes of the slice: x: 4, y: 4, z: 8, core: 2. Of those that a mesh axis runs over, the one named last changes fastest.
Arguments:
- adjacency: int32 [27136, 27136], P('row', 'col'), may hold values from 0 to 3
- degree: int32 [27136], replicated, may hold values from 64 to 511
- cotangent: bfloat16 [27136, 512], P(('row', 'col')), may hold values from -6 to 6
- features: bfloat16 [27136, 512], P('col'), may hold values from -0.029907227 to 0.029907227
- weight: bfloat16 [512, 512], replicated, may hold values from -0.25 to 0.25
Outputs:
- grad_input: bfloat16 [27136, 512], P('col', 'row')
- grad_weight: float32 [512, 512], P('col', 'row')
All inputs are finite; a program needn't handle non-finite values.
Results may differ from a plain program's by a relative error of at most 0.0058.
Values may be sent and summed in bfloat16 or wider, within the bound.
No kernel may reach another device: no remote copies, remote signals or barrier semaphores. Data moves between devices by JAX's collectives and lax.ppermute only.
A program may use at most 128 MiB of HBM per device.

v0:
```python
import jax
import jax.numpy as jnp
from jax import lax
from jax.sharding import Mesh
from jax.sharding import PartitionSpec as P

COL = ("col_0", "col_1")
ROW_COL = ("row", "col_0", "col_1")


def laid_out(blocks, dim):
    lengths = list(blocks.shape[1:])
    lengths[dim] *= blocks.shape[0]
    return jnp.moveaxis(blocks, 0, dim).reshape(lengths)


def gather_in_order(value, axes, turns):
    blocks = value[None]
    for k in turns:
        blocks = lax.all_gather(blocks, axes[k], axis=0, tiled=True)
    current = [lax.axis_size(axes[k]) for k in reversed(turns)]
    blocks = blocks.reshape(*current, *value.shape)
    turned = sorted(range(len(turns)), key=lambda place: turns[len(turns) - 1 - place])
    return blocks.transpose(*turned, *range(len(turns), blocks.ndim)).reshape(-1, *value.shape)


def gather_axes(value, axes, turns, dim):
    return laid_out(gather_in_order(value, axes, turns), dim)


def split_up(value, dim, length):
    lengths = value.shape
    blocks = value.reshape(*lengths[:dim], length, lengths[dim] // length, *lengths[dim + 1 :])
    return jnp.moveaxis(blocks, dim, 0)


def summed_on_arrival(value, axis, dim):
    blocks = split_up(value, dim, lax.axis_size(axis))
    arrived = lax.all_to_all(blocks, axis, split_axis=0, concat_axis=0, tiled=True)
    return arrived.sum(axis=0)


def copy_for_each(value, axis):
    copies = jnp.broadcast_to(value, (lax.axis_size(axis), *value.shape))
    return lax.all_to_all(copies, axis, split_axis=0, concat_axis=0, tiled=True)


def collect(value, axis, dim):
    return laid_out(copy_for_each(value, axis), dim)


def per_device(adjacency, degree, cotangent, features, weight):
    rows_here, cols_here = adjacency.shape
    row_index = lax.axis_index("row")
    col_index = lax.axis_index(COL)
    inv_root = lax.rsqrt(degree.astype(jnp.float32))
    row_scale = lax.dynamic_slice_in_dim(inv_root, row_index * rows_here, rows_here, 0)
    col_scale = lax.dynamic_slice_in_dim(inv_root, col_index * cols_here, cols_here, 0)
    tile = adjacency.astype(jnp.bfloat16)
    width = weight.shape[0]
    scaled = (
        gather_axes(cotangent, COL, (0, 1), 0).astype(jnp.float32) * row_scale[:, None]
    ).astype(jnp.bfloat16)
    partial_sum = lax.dot_general(
        tile, scaled, (((0,), (0,)), ((), ())), preferred_element_type=jnp.float32
    )
    share = width // lax.axis_size("row")
    weight_rows = lax.dynamic_slice_in_dim(weight, row_index * share, share, 0)
    pieces = summed_on_arrival(partial_sum, "row", 1)
    z_columns = (pieces * col_scale[:, None]).astype(jnp.bfloat16)
    grad_z = collect(z_columns, "row", 1)
    grad_input = lax.dot_general(
        grad_z, weight_rows, (((1,), (1,)), ((), ())), preferred_element_type=jnp.float32
    )
    weight_term = lax.dot_general(
        features, z_columns, (((0,), (0,)), ((), ())), preferred_element_type=jnp.float32
    )
    grad_weight = summed_on_arrival(weight_term, COL, 0)
    return (grad_input.astype(jnp.bfloat16), grad_weight)


def solution(mesh):
    torus = Mesh(mesh.devices.reshape(mesh.shape["row"], 4, 8), ("row", "col_0", "col_1"))
    placed = (P("row", COL), P(), P(ROW_COL, None), P(COL, None), P())
    return jax.shard_map(
        per_device,
        mesh=torus,
        in_specs=placed,
        out_specs=(P(COL, "row"), P(COL, "row")),
        check_vma=False,
    )
```

profile of v0, /device:TPU:1, one launch (start us, length us, event | category | flops | bytes accessed | tf_op | source)
XLA Modules:
  0.0 172.6 jit_solution(2381927909333478503)
XLA Ops:
  7.2 0.0 copy-start
  7.2 0.0 all-gather.4.cloned.1.call-start
  7.2 13.1 %all-gather.1 = bf16[4,106,512]{2,1,0:T(8,128)(2,1)} all-gather(bf16[1,106,512]{2,1,0:T(8,128)(2,1)} %bitcast.23), channel_id=2, replica_groups=mesh['row'=8,'col_0'=4,'col_1'=8] {'col_0'}, dimensions={0}, use_global_device_ids=true | all-gather | bytes 542720 | tf_op jit(solution)/shard_map/all_gather | solution.py:20
  20.3 0.0 all-gather.4.cloned.1.call-update
  20.4 0.9 convert_rsqrt_fusion
  21.3 0.1 dynamic_slice.9
  21.4 53.0 %all-gather.4.cloned.1.call-done = bf16[32,106,512]{2,1,0:T(8,128)(2,1)} async-done(((bf16[4,106,512]{2,1,0:T(8,128)(2,1)}), bf16[32,106,512]{2,1,0:T(8,128)(2,1)}) %all-gather.4.cloned.1.call-update) | async-done | bytes 3473424 | tf_op jit(solution)/shard_map/all_gather | solution.py:20
  74.3 6.1 %copy_bitcast_fusion = f32[4,8,106,512]{3,2,1,0:T(8,128)} fusion(bf16[8,4,106,512]{3,2,1,0:T(8,128)(2,1)} %bitcast.21), kind=kLoop, calls=%fused_computation | loop fusion | flops 1736704 | bytes 10420224 | tf_op jit(solution)/shard_map/convert_element_type | solution.py:62
  80.4 6.6 %reshape.23 = f32[3392,512]{1,0:T(8,128)} reshape(f32[4,8,106,512]{3,2,1,0:T(8,128)} %copy_bitcast_fusion) | data formatting | bytes 13893632 | tf_op jit(solution)/shard_map/convert_element_type | solution.py:62
  87.0 9.7 %fusion.3 = f32[848,512]{1,0:T(8,128)S(1)} fusion(f32[3392,512]{1,0:T(8,128)} %reshape.23, f32[3392]{0:T(1024)S(1)} %dynamic_slice.9, s32[3392,848]{0,1:T(8,128)} %param.5), kind=kOutput, calls=%fused_computation.5 | convolution fusion | flops 2951799808 | bytes 20202752 | tf_op jit(solution)/shard_map/dot_general | solution.py:64
  96.7 1.7 copy.11
  98.4 5.1 %all-to-all-start = ((f32[8,848,64]{1,2,0:T(8,128)}), f32[8,848,64]{1,2,0:T(8,128)S(1)}, u32[]{:S(2)}, u32[]{:S(2)}) async-start(f32[8,848,64]{1,2,0:T(8,128)} %bitcast.19), calls=%async_computation | async-start | bytes 3670016 | tf_op jit(solution)/shard_map/all_to_all | solution.py:39
  103.5 0.1 dynamic_slice.10
  103.6 23.3 %all-to-all-done = f32[8,848,64]{1,2,0:T(8,128)S(1)} async-done(((f32[8,848,64]{1,2,0:T(8,128)}), f32[8,848,64]{1,2,0:T(8,128)S(1)}, u32[]{:S(2)}, u32[]{:S(2)}) %all-to-all-start) | async-done | bytes 1736736 | tf_op jit(solution)/shard_map/all_to_all | solution.py:39
  126.9 0.1 reduce_sum.18
  127.0 0.0 copy-done
  127.0 0.3 convolution_bitcast_fusion
  127.3 0.1 copy.12
  127.5 0.2 reshape.29
  127.7 15.8 %all_to_all.15 = f32[32,1,1024]{2,1,0:T(1,128)S(1)} all-to-all(f32[32,1,1024]{2,1,0:T(1,128)S(1)} %reshape.29), channel_id=1, replica_groups=mesh['row'=8,'col_0'=4,'col_1'=8] {'col_0','col_1'}, dimensions={0} | all-to-all | bytes 262144 | tf_op jit(solution)/shard_map/all_to_all | solution.py:39
  143.5 1.0 broadcast_in_dim.9
  144.5 5.8 %all-to-all-start.1 = ((bf16[8,848,64]{1,2,0:T(8,128)(2,1)}), bf16[8,848,64]{1,2,0:T(8,128)(2,1)S(1)}, u32[]{:S(2)}, u32[]{:S(2)}) async-start(bf16[8,848,64]{1,2,0:T(8,128)(2,1)} %broadcast_in_dim.9), calls=%async_computation.1 | async-start | bytes 1835008 | tf_op jit(solution)/shard_map/all_to_all | solution.py:45
  150.3 0.5 broadcast.2
  150.9 0.9 reduce
  151.8 0.1 reshape.30
  151.9 0.6 reduce_sum.19
  152.6 11.4 %all-to-all-done.1 = bf16[8,848,64]{1,2,0:T(8,128)(2,1)S(1)} async-done(((bf16[8,848,64]{1,2,0:T(8,128)(2,1)}), bf16[8,848,64]{1,2,0:T(8,128)(2,1)S(1)}, u32[]{:S(2)}, u32[]{:S(2)}) %all-to-all-start.1) | async-done | bytes 868384 | tf_op jit(solution)/shard_map/all_to_all | solution.py:45
  163.9 1.8 %convolution_convert_fusion = bf16[848,64]{0,1:T(8,128)(2,1)} fusion(bf16[848,512]{0,1:T(8,128)(2,1)S(1)} %bitcast.20, bf16[512,512]{1,0:T(8,128)(2,1)} %param.9, s32[]{:T(128)S(6)} %select_n.11), kind=kOutput, calls=%fused_computation.6 | convolution fusion | flops 55628800 | bytes 1042436 | tf_op jit(solution)/shard_map/dot_general | solution.py:72
  (1 shorter events, 0.0 us)
Async XLA Ops:
  7.2 119.9 %copy-start = (bf16[848,512]{1,0:T(8,128)(2,1)S(1)}, bf16[848,512]{1,0:T(8,128)(2,1)}, u32[]{:S(2)}) copy-start(bf16[848,512]{1,0:T(8,128)(2,1)} %param.8) | copy-start | bytes 2605060
  7.2 67.2 %all-gather.4.cloned.1.call-start = ((), (), s32[]{:S(2)}) async-start(), calls=%async_computation.3 | async-start | bytes 4128768 | tf_op jit(solution)/shard_map/all_gather | solution.py:20
  98.4 28.5 %all-to-all-start = ((f32[8,848,64]{1,2,0:T(8,128)}), f32[8,848,64]{1,2,0:T(8,128)S(1)}, u32[]{:S(2)}, u32[]{:S(2)}) async-start(f32[8,848,64]{1,2,0:T(8,128)} %bitcast.19), calls=%async_computation | async-start | bytes 3670016 | tf_op jit(solution)/shard_map/all_to_all | solution.py:39
  144.5 19.4 %all-to-all-start.1 = ((bf16[8,848,64]{1,2,0:T(8,128)(2,1)}), bf16[8,848,64]{1,2,0:T(8,128)(2,1)S(1)}, u32[]{:S(2)}, u32[]{:S(2)}) async-start(bf16[8,848,64]{1,2,0:T(8,128)(2,1)} %broadcast_in_dim.9), calls=%async_computation.1 | async-start | bytes 1835008 | tf_op jit(solution)/shard_map/all_to_all | solution.py:45
Sparse Core Ops, SparseCore 0:
  20.5 53.8 all-gather.3
where the time goes:
time: 173 us
  waiting for transfers between devices  87.7 us (51%)
  blocking collectives  28.9 us (17%)
  between operations  14.1 us (8%)
  matrix products  11.7 us (7%)
  starting transfers between devices  11 us (6%)
  local copies, waits for them, and re-layouts  10.5 us (6%)
  other arithmetic  8.69 us (5%)
    all_gather x1, waiting for transfers between devices, gather_in_order(): blocks = lax.all_gather(blocks, axes[k], axis=0, tiled=True)  53 us
    all_to_all x1, waiting for transfers between devices, summed_on_arrival(): lax.all_to_all(blocks, axis, split_axis=0, concat_axis=0, tiled=True)  23.3 us
    all_to_all x1, blocking collectives, summed_on_arrival(): lax.all_to_all(blocks, axis, split_axis=0, concat_axis=0, tiled=True)  15.8 us
    all_gather x1, blocking collectives, gather_in_order(): blocks = lax.all_gather(blocks, axes[k], axis=0, tiled=True)  13.1 us
    all_to_all x1, waiting for transfers between devices, copy_for_each(): return lax.all_to_all(copies, axis, split_axis=0, concat_axis=0, tiled=True)  11.4 us
    dot_general x1, matrix products, per_device(): lax.dot_general(tile, scaled, (((0,), (0,)), ((), ())), preferred_element...  9.67 us
    convert_element_type x1, local copies, waits for them, and re-layouts, per_device(): gather_axes(cotangent, COL, (0, 1), 0).astype(jnp.float32)  6.6 us
    convert_element_type x1, other arithmetic, per_device(): gather_axes(cotangent, COL, (0, 1), 0).astype(jnp.float32)  6.06 us
  transfers between devices with their start and end apart: 3, of which 3 were waited for; matrix products, arithmetic and copies ran while one was open for 2% of the time, Pallas kernels for 0%

commit v1 on v0

v1 whole, which is shorter than its diff:
```python
import functools

import jax
import jax.numpy as jnp
from jax import lax
from jax.experimental import pallas as pl
from jax.experimental.pallas import tpu as pltpu
from jax.sharding import Mesh
from jax.sharding import PartitionSpec as P


X, Z = "col_0", "col_1"
COL = (X, Z)
ROW_COL = ("row", X, Z)
NT = (((1,), (1,)), ((), ()))
TN = (((0,), (0,)), ((), ()))
CORES = 2

VMEM = pl.BlockSpec(memory_space=pltpu.VMEM)
SMEM = pl.BlockSpec(memory_space=pltpu.SMEM)


def shifted(value, axis, step):
    n = lax.axis_size(axis)
    return lax.ppermute(value, axis, [(i, (i + step) % n) for i in range(n)])


def call(body, out, args, scratch=(), smem=1, flops=1 << 20, limit=16):
    return pl.pallas_call(
        body,
        out_shape=out,
        in_specs=[SMEM] * smem + [VMEM] * (len(args) - smem),
        out_specs=jax.tree.map(lambda _: VMEM, out),
        scratch_shapes=list(scratch),
        compiler_params=pltpu.CompilerParams(vmem_limit_bytes=limit << 20),
        cost_estimate=pl.CostEstimate(flops=flops, bytes_accessed=1 << 20, transcendentals=0),
    )(*args)


def arrange_kernel(steps, me_ref, *refs):
    *pieces, out_ref = refs
    n = out_ref.shape[0]
    for step, ref in zip(steps, pieces):
        out_ref[lax.rem(me_ref[0] + (step + n), n)] = ref[...]


def convert_kernel(tile_ref, out_ref):
    out_ref[...] = tile_ref[...].astype(jnp.float32).astype(jnp.bfloat16)


def product(x_major, me_ref, tile_ref, scale_ref, refs, slots, rows):
    n, m, length, _ = slots.shape
    me = me_ref[0]
    own, _, _ = refs[:3]
    slots[me] = own[...]
    for step in range(1, n // 2):
        up, down = refs[2 * step - 1], refs[2 * step]
        slots[lax.rem(me + (n - step), n)] = up[...]
        slots[lax.rem(me + step, n)] = down[...]
    across = lax.rem(me + n // 2, n)
    slots[across, : m // 2] = refs[-2][...]
    slots[across, m // 2 :] = refs[-1][...]
    for i in range(n):
        for j in range(m):
            k = i * m + j if x_major else j * n + i
            rows[pl.ds(k * length, length), :] = slots[i, j].astype(jnp.float32)
    total = jnp.dot(
        tile_ref[...], rows[...].astype(jnp.bfloat16), preferred_element_type=jnp.float32
    )
    return (total * scale_ref[...]).astype(jnp.bfloat16)


def first_kernel(me_ref, tile_ref, scale_ref, features_ref, *rest):
    *refs, out_ref, r_ref, slots, rows = rest
    out_ref[...] = product(False, me_ref, tile_ref, scale_ref, refs, slots, rows)
    r_ref[...] = lax.dot_general(
        out_ref[...], features_ref[...], TN, preferred_element_type=jnp.float32
    )


def parted(core, held, keep_ref, send_ref):
    for y in range(keep_ref.shape[0]):
        keep_ref[y] = held[CORES * y + core]
        send_ref[y] = held[CORES * y + (CORES - 1 - core)].astype(send_ref.dtype)


def second_kernel(me_ref, tile_ref, scale_ref, features_ref, r_first_ref, *rest):
    *refs, out_ref, keep_ref, send_ref, slots, rows, held = rest
    out_ref[...] = product(True, me_ref, tile_ref, scale_ref, refs, slots, rows)
    r = lax.dot_general(
        out_ref[...], features_ref[...], TN, preferred_element_type=jnp.float32
    )
    n_row, share, width = held.shape
    held[: n_row // 2] = r_first_ref[...].reshape(n_row // 2, share, width)
    held[n_row // 2 :] = r.reshape(n_row // 2, share, width)
    parted(me_ref[1], held, keep_ref, send_ref)


def q_kernel(me_ref, first_ref, second_ref, weight_ref, keep_ref, send_ref, held):
    half = first_ref.shape[1]
    q = lax.dot_general(
        weight_ref[:, :half], first_ref[...], NT, preferred_element_type=jnp.float32
    )
    q += lax.dot_general(
        weight_ref[:, half:], second_ref[...], NT, preferred_element_type=jnp.float32
    )
    held[...] = q.reshape(held.shape)
    parted(me_ref[0], held, keep_ref, send_ref)


def join_kernel(me_ref, keep_ref, got_ref, own_ref, *send_refs):
    n, me = keep_ref.shape[0], me_ref[0]
    own_ref[...] = keep_ref[me] + got_ref[me].astype(jnp.float32)
    for step, ref in enumerate(send_refs, 1):
        to = lax.rem(me + step, n)
        ref[...] = (keep_ref[to] + got_ref[to].astype(jnp.float32)).astype(ref.dtype)


def added(own_ref, refs):
    total = own_ref[...]
    for ref in refs:
        total += ref[...].astype(jnp.float32)
    return total


def pack_kernel(own_ref, *rest):
    *refs, out_ref = rest
    total = added(own_ref, refs)
    n_col, lines, _ = out_ref.shape
    share = total.shape[0]
    blocks = total.T.reshape(n_col, 2 * lines, share)
    out_ref[:, :, :share] = blocks[:, :lines]
    out_ref[:, :, share:] = blocks[:, lines:]


def unpack_kernel(pieces_ref, out_ref):
    lines, share = pieces_ref.shape[1], out_ref.shape[1]
    total = pieces_ref[...].sum(axis=0)
    out_ref[:lines, :] = total[:, :share]
    out_ref[lines:, :] = total[:, share:]


def sum_kernel(own_ref, *rest):
    *refs, out_ref = rest
    out_ref[...] = added(own_ref, refs).astype(out_ref.dtype)


def over_rows(me, keep, send, n_y):
    _, share, length = keep.shape
    n = n_y * CORES
    got = lax.ppermute(send, "row", [(i, i ^ 1) for i in range(n)])
    block = functools.partial(jax.ShapeDtypeStruct, (share, length))
    own, *parts = call(
        join_kernel, (block(jnp.float32),) + (block(jnp.bfloat16),) * (n_y - 1), (me, keep, got)
    )
    arrived = [
        lax.ppermute(part, "row", [(i, (i + CORES * step) % n) for i in range(n)])
        for step, part in enumerate(parts, 1)
    ]
    return own, arrived


def per_device(adjacency, degree, cotangent, features, weight):
    rows_here, cols_here = adjacency.shape
    length, width = cotangent.shape
    half = width // 2
    row = lax.axis_index("row")
    x, z = lax.axis_index(X), lax.axis_index(Z)
    nx, nz = lax.axis_size(X), lax.axis_size(Z)
    n_row = lax.axis_size("row")
    n_y = n_row // CORES
    col = lax.axis_index(COL)
    y, core = row // CORES, row % CORES

    def inv_root(start, size):
        return lax.rsqrt(lax.dynamic_slice_in_dim(degree, start, size, 0).astype(jnp.float32))

    scaled = (
        cotangent.astype(jnp.float32)
        * inv_root(row * rows_here + col * length, length)[:, None]
    ).astype(jnp.bfloat16)
    mine_a, mine_b = scaled[:, :half], scaled[:, half:]
    tile = call(
        convert_kernel,
        jax.ShapeDtypeStruct((cols_here, rows_here), jnp.bfloat16),
        (adjacency.T,),
        smem=0,
        limit=40,
    )
    col_scale = inv_root(col * cols_here, cols_here)[:, None]

    unit = functools.partial(jax.ShapeDtypeStruct, dtype=jnp.bfloat16)
    near = [shifted(mine_a, X, s) for s in range(1, nx)]
    a = call(
        functools.partial(arrange_kernel, [0] + [-s for s in range(1, nx)]),
        unit((nx, length, half)),
        (x.reshape(1), mine_a, *near),
    )
    far = [shifted(mine_b, Z, s) for s in range(1, nz)]
    b = call(
        functools.partial(arrange_kernel, [0] + [-s for s in range(1, nz)]),
        unit((nz, length, half)),
        (z.reshape(1), mine_b, *far),
    )

    def ring(own, axis):
        n = lax.axis_size(axis)
        middle = own.shape[0] // 2
        units, up, down = [own], own, own
        for step in range(1, n // 2 + 1):
            if step == n // 2:
                up, down = up[:middle], down[middle:]
            up = shifted(up, axis, 1)
            down = shifted(down, axis, -1)
            units += [up, down]
        return units

    a_units = ring(a, Z)
    b_units = ring(b, X)

    flops = 2 * rows_here * cols_here * half
    rows_buffer = pltpu.VMEM((rows_here, half), jnp.float32)
    first, r_first = call(
        first_kernel,
        (unit((cols_here, half)), jax.ShapeDtypeStruct((half, width), jnp.float32)),
        (z.reshape(1), tile, col_scale, features, *a_units),
        scratch=(pltpu.VMEM((nz, nx, length, half), jnp.bfloat16), rows_buffer),
        flops=flops,
        limit=32,
    )
    share = width // n_row
    second, r_keep, r_send = call(
        second_kernel,
        (
            unit((cols_here, half)),
            jax.ShapeDtypeStruct((n_y, share, width), jnp.float32),
            unit((n_y, share, width)),
        ),
        (jnp.stack([x, core]), tile, col_scale, features, r_first, *b_units),
        scratch=(
            pltpu.VMEM((nx, nz, length, half), jnp.bfloat16),
            rows_buffer,
            pltpu.VMEM((n_row, share, width), jnp.float32),
        ),
        flops=flops,
        limit=32,
    )
    q_keep, q_send = call(
        q_kernel,
        (
            jax.ShapeDtypeStruct((n_y, share, cols_here), jnp.float32),
            unit((n_y, share, cols_here)),
        ),
        (core.reshape(1), first, second, weight),
        scratch=(pltpu.VMEM((n_row, share, cols_here), jnp.float32),),
        flops=2 * cols_here * width * width,
    )
    r_own, r_parts = over_rows(y.reshape(1), r_keep, r_send, n_y)
    q_own, q_parts = over_rows(y.reshape(1), q_keep, q_send, n_y)

    n_col = nx * nz
    lines = width // n_col // 2
    packed = call(
        pack_kernel,
        jax.ShapeDtypeStruct((n_col, lines, 2 * share), jnp.float32),
        (r_own, *r_parts),
        smem=0,
    )
    w_pieces = lax.all_to_all(packed, COL, split_axis=0, concat_axis=0, tiled=True)
    grad_weight = call(
        unpack_kernel, jax.ShapeDtypeStruct((2 * lines, share), jnp.float32), (w_pieces,), smem=0
    )
    grad_input = call(sum_kernel, unit((share, cols_here)), (q_own, *q_parts), smem=0).T
    return (grad_input, grad_weight)


def solution(mesh):
    torus = Mesh(mesh.devices.reshape(mesh.shape["row"], 4, 8), ("row", X, Z))
    placed = (P("row", COL), P(), P(ROW_COL, None), P(COL, None), P())
    return jax.shard_map(
        per_device,
        mesh=torus,
        in_specs=placed,
        out_specs=(P(COL, "row"), P(COL, "row")),
        check_vma=False,
    )
```

time: 173 us -> 107 us (0.62)
  waiting for transfers between devices: 87.7 us -> 18.7 us
  starting transfers between devices: 11 us -> 66.2 us
  blocking collectives: 28.9 us -> 0 us
  Pallas kernels: 0 us -> 15.5 us
  between operations: 14.1 us -> 0.91 us
  matrix products: 11.7 us -> 0 us
  local copies, waits for them, and re-layouts: 10.5 us -> 1.63 us
  other arithmetic: 8.69 us -> 2.68 us
    ppermute x0 -> x30, starting transfers between devices: none -> 59 us  [the longest x22 39.1 us: shifted(): return lax.ppermute(value, axis, [(i, (i + step) % n) for i in range(n)])]
    all_gather x1 -> x0, waiting for transfers between devices: 53 us -> none  [gather_in_order(): blocks = lax.all_gather(blocks, axes[k], axis=0, tiled=True)]
    all_to_all x2 -> x1, waiting for transfers between devices: 34.7 us -> 1.16 us  [per_device(): lax.all_to_all(packed, COL, split_axis=0, concat_axis=0, tiled=True)]
    ppermute x0 -> x30, waiting for transfers between devices: none -> 17.5 us  [the longest x22 11.4 us: shifted(): return lax.ppermute(value, axis, [(i, (i + step) % n) for i in range(n)])]
    all_to_all x1 -> x0, blocking collectives: 15.8 us -> none  [summed_on_arrival(): lax.all_to_all(blocks, axis, split_axis=0, concat_axis=0, tiled=True)]
    pallas_call x0 -> x11, Pallas kernels: none -> 15.5 us  [call(): pl.pallas_call(body, out_shape=out, in_specs=[SMEM] * smem + [VMEM] * (le...]
    all_gather x1 -> x0, blocking collectives: 13.1 us -> none  [gather_in_order(): blocks = lax.all_gather(blocks, axes[k], axis=0, tiled=True)]
    dot_general x3 -> x0, matrix products: 11.7 us -> none  [the longest x1 9.67 us: per_device(): lax.dot_general(tile, scaled, (((0,), (0,)), ((), ())), preferred_element...]
  transfers between devices with their start and end apart: 3 -> 31, of which waited for: 3 -> 17; matrix products, arithmetic and copies ran while one was open for 2% -> 1% of each run, Pallas kernels for 0% -> 11%
where the time goes in v1:
time: 107 us; the launch traced here: 106 us
  starting transfers between devices  66.2 us (62%)
  waiting for transfers between devices  18.7 us (17%)
  Pallas kernels  15.5 us (14%)
  other arithmetic  2.68 us (3%)
  local copies, waits for them, and re-layouts  1.63 us (2%)
    ppermute x22, starting transfers between devices, shifted(): return lax.ppermute(value, axis, [(i, (i + step) % n) for i in range(n)])  39.1 us
    pallas_call x11, Pallas kernels, call(): pl.pallas_call(body, out_shape=out, in_specs=[SMEM] * smem + [VMEM] * (le...  15.5 us
    ppermute x22, waiting for transfers between devices, shifted(): return lax.ppermute(value, axis, [(i, (i + step) % n) for i in range(n)])  11.4 us
    ppermute x2, starting transfers between devices, over_rows(): got = lax.ppermute(send, 'row', [(i, i ^ 1) for i in range(n)])  11.1 us
    ppermute x6, starting transfers between devices, over_rows(): lax.ppermute(part, 'row', [(i, (i + CORES * step) % n) for i in range(n)])  8.68 us
    all_to_all x1, starting transfers between devices, per_device(): lax.all_to_all(packed, COL, split_axis=0, concat_axis=0, tiled=True)  7.26 us
    ppermute x6, waiting for transfers between devices, over_rows(): lax.ppermute(part, 'row', [(i, (i + CORES * step) % n) for i in range(n)])  5.9 us
  transfers between devices with their start and end apart: 31, of which 17 were waited for; matrix products, arithmetic and copies ran while one was open for 1% of the time, Pallas kernels for 11%

profile of v1, /device:TPU:1, one launch (start us, length us, event | category | flops | bytes accessed | tf_op | source)
XLA Modules:
  0.0 105.6 jit_solution(9009588300007695586)
XLA Ops:
  0.7 0.9 convert_rsqrt_fusion.1
  1.5 1.0 multiply_convert_fusion
  2.5 2.1 %collective-permute-start = (bf16[106,256]{1,0:T(8,128)(2,1)S(1)}, bf16[106,256]{1,0:T(8,128)(2,1)S(1)}, u32[]{:S(2)}, u32[]{:S(2)}) collective-permute-start(bf16[106,256]{1,0:T(8,128)(2,1)S(1)} %get-tuple-element.33.refs_0_), channel_id=1, source_target_pairs={{0,8},{8,16},{16,24},{24,0},{1,9},{9,17},{17,25},{25,1},{2,10},{10... | collective-permute-start | bytes 162824 | tf_op jit(solution)/shard_map/ppermute | solution.py:25
  4.6 2.5 %collective-permute-start.1 = (bf16[106,256]{1,0:T(8,128)(2,1)S(1)}, bf16[106,256]{1,0:T(8,128)(2,1)S(1)}, u32[]{:S(2)}, u32[]{:S(2)}) collective-permute-start(bf16[106,256]{1,0:T(8,128)(2,1)S(1)} %get-tuple-element.33.refs_0_), channel_id=1, source_target_pairs={{0,16},{8,24},{16,0},{24,8},{1,17},{9,25},{17,1},{25,9},{2,18},{10... | collective-permute-start | bytes 162824 | tf_op jit(solution)/shard_map/ppermute | solution.py:25
  7.1 1.2 %collective-permute-start.2 = (bf16[106,256]{1,0:T(8,128)(2,1)S(1)}, bf16[106,256]{1,0:T(8,128)(2,1)S(1)}, u32[]{:S(2)}, u32[]{:S(2)}) collective-permute-start(bf16[106,256]{1,0:T(8,128)(2,1)S(1)} %get-tuple-element.33.refs_0_), channel_id=1, source_target_pairs={{0,24},{8,0},{16,8},{24,16},{1,25},{9,1},{17,9},{25,17},{2,26},{10... | collective-permute-start | bytes 162824 | tf_op jit(solution)/shard_map/ppermute | solution.py:25
  8.2 1.1 %collective-permute-done.1.refs_2_ = bf16[106,256]{1,0:T(8,128)(2,1)S(1)} collective-permute-done((bf16[106,256]{1,0:T(8,128)(2,1)S(1)}, bf16[106,256]{1,0:T(8,128)(2,1)S(1)}, u32[]{:S(2)}, u32[]{:S(2)}) %collective-permute-start.1) | collective-permute-done | bytes 54304 | tf_op jit(solution)/shard_map/ppermute | solution.py:25
  9.3 1.1 collective-permute-done.2.refs_3_
  10.4 1.9 %collective-permute-start.3 = (bf16[4,106,256]{2,1,0:T(8,128)(2,1)S(1)}, bf16[4,106,256]{2,1,0:T(8,128)(2,1)S(1)}, u32[]{:S(2)}, u32[]{:S(2)}) collective-permute-start(bf16[4,106,256]{2,1,0:T(8,128)(2,1)S(1)} %shard_map.69.rest_0_), channel_id=1, source_target_pairs={{0,1},{1,2},{2,3},{3,4},{4,5},{5,6},{6,7},{7,0},{8,9},{9,10},{10,1... | collective-permute-start | bytes 651272 | tf_op jit(solution)/shard_map/ppermute | solution.py:25
  12.3 4.0 %collective-permute-start.4 = (bf16[4,106,256]{2,1,0:T(8,128)(2,1)S(1)}, bf16[4,106,256]{2,1,0:T(8,128)(2,1)S(1)}, u32[]{:S(2)}, u32[]{:S(2)}) collective-permute-start(bf16[4,106,256]{2,1,0:T(8,128)(2,1)S(1)} %shard_map.69.rest_0_), channel_id=1, source_target_pairs={{0,7},{1,0},{2,1},{3,2},{4,3},{5,4},{6,5},{7,6},{8,15},{9,8},{10,9... | collective-permute-start | bytes 651272 | tf_op jit(solution)/shard_map/ppermute | solution.py:25
  16.3 1.8 %collective-permute-start.12 = (bf16[106,256]{1,0:T(8,128)(2,1)S(1)}, bf16[106,256]{1,0:T(8,128)(2,1)S(1)}, u32[]{:S(2)}, u32[]{:S(2)}) collective-permute-start(bf16[106,256]{1,0:T(8,128)(2,1)S(1)} %get-tuple-element.32.refs_0_), channel_id=1, source_target_pairs={{0,2},{1,3},{2,4},{3,5},{4,6},{5,7},{6,0},{7,1},{8,10},{9,11},{10,... | collective-permute-start | bytes 162824 | tf_op jit(solution)/shard_map/ppermute | solution.py:25
  18.1 2.4 %collective-permute-start.13 = (bf16[106,256]{1,0:T(8,128)(2,1)S(1)}, bf16[106,256]{1,0:T(8,128)(2,1)S(1)}, u32[]{:S(2)}, u32[]{:S(2)}) collective-permute-start(bf16[106,256]{1,0:T(8,128)(2,1)S(1)} %get-tuple-element.32.refs_0_), channel_id=1, source_target_pairs={{0,3},{1,4},{2,5},{3,6},{4,7},{5,0},{6,1},{7,2},{8,11},{9,12},{10,... | collective-permute-start | bytes 162824 | tf_op jit(solution)/shard_map/ppermute | solution.py:25
  20.5 1.0 collective-permute-done.11.refs_1_
  21.5 4.2 %collective-permute-start.14 = (bf16[106,256]{1,0:T(8,128)(2,1)S(1)}, bf16[106,256]{1,0:T(8,128)(2,1)S(1)}, u32[]{:S(2)}, u32[]{:S(2)}) collective-permute-start(bf16[106,256]{1,0:T(8,128)(2,1)S(1)} %get-tuple-element.32.refs_0_), channel_id=1, source_target_pairs={{0,4},{1,5},{2,6},{3,7},{4,0},{5,1},{6,2},{7,3},{8,12},{9,13},{10,... | collective-permute-start | bytes 162824 | tf_op jit(solution)/shard_map/ppermute | solution.py:25
  25.7 1.7 %collective-permute-start.15 = (bf16[106,256]{1,0:T(8,128)(2,1)S(1)}, bf16[106,256]{1,0:T(8,128)(2,1)S(1)}, u32[]{:S(2)}, u32[]{:S(2)}) collective-permute-start(bf16[106,256]{1,0:T(8,128)(2,1)S(1)} %get-tuple-element.32.refs_0_), channel_id=1, source_target_pairs={{0,5},{1,6},{2,7},{3,0},{4,1},{5,2},{6,3},{7,4},{8,13},{9,14},{10,... | collective-permute-start | bytes 162824 | tf_op jit(solution)/shard_map/ppermute | solution.py:25
  27.4 2.8 %collective-permute-start.16 = (bf16[106,256]{1,0:T(8,128)(2,1)S(1)}, bf16[106,256]{1,0:T(8,128)(2,1)S(1)}, u32[]{:S(2)}, u32[]{:S(2)}) collective-permute-start(bf16[106,256]{1,0:T(8,128)(2,1)S(1)} %get-tuple-element.32.refs_0_), channel_id=1, source_target_pairs={{0,6},{1,7},{2,0},{3,1},{4,2},{5,3},{6,4},{7,5},{8,14},{9,15},{10,... | collective-permute-start | bytes 162824 | tf_op jit(solution)/shard_map/ppermute | solution.py:25
  30.2 0.4 collective-permute-start.17
  30.6 0.9 collective-permute-done.15.refs_5_
  31.4 1.1 %collective-permute-done.16.refs_6_ = bf16[106,256]{1,0:T(8,128)(2,1)S(1)} collective-permute-done((bf16[106,256]{1,0:T(8,128)(2,1)S(1)}, bf16[106,256]{1,0:T(8,128)(2,1)S(1)}, u32[]{:S(2)}, u32[]{:S(2)}) %collective-permute-start.16) | collective-permute-done | bytes 54304 | tf_op jit(solution)/shard_map/ppermute | solution.py:25
  32.5 1.4 %collective-permute-done.17.refs_7_ = bf16[106,256]{1,0:T(8,128)(2,1)S(1)} collective-permute-done((bf16[106,256]{1,0:T(8,128)(2,1)S(1)}, bf16[106,256]{1,0:T(8,128)(2,1)S(1)}, u32[]{:S(2)}, u32[]{:S(2)}) %collective-permute-start.17) | collective-permute-done | bytes 54304 | tf_op jit(solution)/shard_map/ppermute | solution.py:25
  34.0 0.1 collective-permute-start.18
  34.1 2.7 %collective-permute-start.19 = (bf16[8,106,256]{2,1,0:T(8,128)(2,1)S(1)}, bf16[8,106,256]{2,1,0:T(8,128)(2,1)S(1)}, u32[]{:S(2)}, u32[]{:S(2)}) collective-permute-start(bf16[8,106,256]{2,1,0:T(8,128)(2,1)S(1)} %shard_map.71.rest_0_), channel_id=1, source_target_pairs={{0,24},{8,0},{16,8},{24,16},{1,25},{9,1},{17,9},{25,17},{2,26},{10... | collective-permute-start | bytes 1302536 | tf_op jit(solution)/shard_map/ppermute | solution.py:25
  36.7 0.1 collective-permute-start.5
  36.8 0.7 copy-done.1
  37.5 2.6 %collective-permute-start.6 = (bf16[4,106,256]{2,1,0:T(8,128)(2,1)S(1)}, bf16[4,106,256]{2,1,0:T(8,128)(2,1)}, u32[]{:S(2)}, u32[]{:S(2)}) collective-permute-start(bf16[4,106,256]{2,1,0:T(8,128)(2,1)S(1)} %collective-permute-done.4.rest_2_), channel_id=1, source_target_pairs={{0,7},{1,0},{2,1},{3,2},{4,3},{5,4},{6,5},{7,6},{8,15},{9,8},{10,9... | collective-permute-start | bytes 651272 | tf_op jit(solution)/shard_map/ppermute | solution.py:25
  40.1 0.7 copy-done.3
  40.8 2.1 %collective-permute-done.5.rest_3_ = bf16[4,106,256]{2,1,0:T(8,128)(2,1)} collective-permute-done((bf16[4,106,256]{2,1,0:T(8,128)(2,1)S(1)}, bf16[4,106,256]{2,1,0:T(8,128)(2,1)}, u32[]{:S(2)}, u32[]{:S(2)}) %collective-permute-start.5) | collective-permute-done | bytes 217120 | tf_op jit(solution)/shard_map/ppermute | solution.py:25
  42.9 0.0 collective-permute-start.7
  42.9 0.1 collective-permute-done.6.rest_4_
  43.1 3.2 %collective-permute-start.8 = (bf16[4,106,256]{2,1,0:T(8,128)(2,1)}, bf16[4,106,256]{2,1,0:T(8,128)(2,1)S(1)}, u32[]{:S(2)}, u32[]{:S(2)}) collective-permute-start(bf16[4,106,256]{2,1,0:T(8,128)(2,1)} %collective-permute-done.6.rest_4_), channel_id=1, source_target_pairs={{0,7},{1,0},{2,1},{3,2},{4,3},{5,4},{6,5},{7,6},{8,15},{9,8},{10,9... | collective-permute-start | bytes 651272 | tf_op jit(solution)/shard_map/ppermute | solution.py:25
  46.3 0.8 convert_rsqrt_fusion
  47.1 0.2 broadcast_in_dim.5.scale_ref
  47.3 5.0 %shard_map.68.tile_ref = bf16[848,3392]{1,0:T(8,128)(2,1)S(1)} custom-call(s32[848,3392]{1,0:T(8,128)} %bitcast.6), custom_call_target="tpu_custom_call" | custom-call | flops 1048576 | bytes 1048576 | tf_op jit(solution)/shard_map/pallas_call | solution.py:29
  52.2 0.0 copy-start.5
  52.3 0.1 collective-permute-start.20
  52.4 2.7 %collective-permute-start.21 = (bf16[4,106,256]{2,1,0:T(8,128)(2,1)S(1)}, bf16[4,106,256]{2,1,0:T(8,128)(2,1)S(1)}, u32[]{:S(2)}, u32[]{:S(2)}) collective-permute-start(bf16[4,106,256]{2,1,0:T(8,128)(2,1)S(1)} %slice.29), channel_id=1, source_target_pairs={{0,24},{8,0},{16,8},{24,16},{1,25},{9,1},{17,9},{25,17},{2,26},{10... | collective-permute-start | bytes 651272 | tf_op jit(solution)/shard_map/ppermute | solution.py:25
  55.2 0.1 collective-permute-start.9
  55.3 2.7 %collective-permute-start.10 = (bf16[2,106,256]{2,1,0:T(8,128)(2,1)S(1)}, bf16[2,106,256]{2,1,0:T(8,128)(2,1)S(1)}, u32[]{:S(2)}, u32[]{:S(2)}) collective-permute-start(bf16[2,106,256]{2,1,0:T(8,128)(2,1)S(1)} %slice.26), channel_id=1, source_target_pairs={{0,7},{1,0},{2,1},{3,2},{4,3},{5,4},{6,5},{7,6},{8,15},{9,8},{10,9... | collective-permute-start | bytes 325640 | tf_op jit(solution)/shard_map/ppermute | solution.py:25
  58.0 0.1 pad_add_fusion.me_ref
  58.1 2.4 %collective-permute-done.9.rest_7_ = bf16[2,106,256]{2,1,0:T(8,128)(2,1)S(1)} collective-permute-done((bf16[2,106,256]{2,1,0:T(8,128)(2,1)S(1)}, bf16[2,106,256]{2,1,0:T(8,128)(2,1)S(1)}, u32[]{:S(2)}, u32[]{:S(2)}) %collective-permute-start.9) | collective-permute-done | bytes 108576 | tf_op jit(solution)/shard_map/ppermute | solution.py:25
  60.5 0.2 collective-permute-done.10.rest_8_
  60.7 3.8 %shard_map.70 = (bf16[848,256]{1,0:T(8,128)(2,1)S(1)}, f32[256,512]{1,0:T(8,128)S(1)}) custom-call(s32[1]{0:T(128)} %bitcast.2.me_ref, bf16[848,3392]{1,0:T(8,128)(2,1)S(1)} %shard_map.68.tile_ref, f32[848,1]{1,0:T(8,128)S(1)} %broadcast_in_dim.5.scale_ref, bf16[848,512]{1,0:T(8,128)(2,1)S(1)} %copy-done, bf16[4,106,256]{2,1,0:T(8,128)(2,1)S(1)} %shard_map.69.rest_0_, ...), custom_call_target="tpu_custom_call" | custom-call | flops 1472724992 | bytes 1048576 | tf_op jit(solution)/shard_map/pallas_call | solution.py:29
  64.5 3.4 %shard_map.72 = (bf16[848,256]{1,0:T(8,128)(2,1)S(1)}, f32[4,64,512]{2,1,0:T(8,128)S(1)}, bf16[4,64,512]{2,1,0:T(8,128)(2,1)S(1)}) custom-call(s32[2]{0:T(128)S(1)} %pad_add_fusion.me_ref, bf16[848,3392]{1,0:T(8,128)(2,1)S(1)} %shard_map.68.tile_ref, f32[848,1]{1,0:T(8,128)S(1)} %broadcast_in_dim.5.scale_ref, bf16[848,512]{1,0:T(8,128)(2,1)S(1)} %copy-done, ...), custom_call_target="tpu_custom_call" | custom-call | flops 1472724992 | bytes 1048576 | tf_op jit(solution)/shard_map/pallas_call | solution.py:29
  68.0 11.0 %collective-permute-start.26 = (bf16[4,64,512]{2,1,0:T(8,128)(2,1)S(1)}, bf16[4,64,512]{2,1,0:T(8,128)(2,1)S(1)}, u32[]{:S(2)}, u32[]{:S(2)}) collective-permute-start(bf16[4,64,512]{2,1,0:T(8,128)(2,1)S(1)} %get-tuple-element.27), channel_id=1, source_target_pairs={{0,32},{32,0},{64,96},{96,64},{128,160},{160,128},{192,224},{224,1... | collective-permute-start | bytes 786440 | tf_op jit(solution)/shard_map/ppermute | solution.py:151
  79.0 0.8 shard_map.73
  79.8 0.1 collective-permute-start.22
  80.0 0.2 collective-permute-done.26.got_ref
  80.1 0.1 shard_map.76
  80.2 1.4 %collective-permute-start.27 = (bf16[64,512]{1,0:T(8,128)(2,1)S(1)}, bf16[64,512]{1,0:T(8,128)(2,1)S(1)}, u32[]{:S(2)}, u32[]{:S(2)}) collective-permute-start(bf16[64,512]{1,0:T(8,128)(2,1)S(1)} %get-tuple-element.29), channel_id=1, source_target_pairs={{0,64},{32,96},{64,128},{96,160},{128,192},{160,224},{192,0},{224,... | collective-permute-start | bytes 196616 | tf_op jit(solution)/shard_map/ppermute | solution.py:157
  81.6 2.6 %collective-permute-start.28 = (bf16[64,512]{1,0:T(8,128)(2,1)S(1)}, bf16[64,512]{1,0:T(8,128)(2,1)S(1)}, u32[]{:S(2)}, u32[]{:S(2)}) collective-permute-start(bf16[64,512]{1,0:T(8,128)(2,1)S(1)} %get-tuple-element.30), channel_id=1, source_target_pairs={{0,128},{32,160},{64,192},{96,224},{128,0},{160,32},{192,64},{224,... | collective-permute-start | bytes 196616 | tf_op jit(solution)/shard_map/ppermute | solution.py:157
  84.2 1.1 %collective-permute-start.29 = (bf16[64,512]{1,0:T(8,128)(2,1)S(1)}, bf16[64,512]{1,0:T(8,128)(2,1)S(1)}, u32[]{:S(2)}, u32[]{:S(2)}) collective-permute-start(bf16[64,512]{1,0:T(8,128)(2,1)S(1)} %get-tuple-element.31), channel_id=1, source_target_pairs={{0,192},{32,224},{64,0},{96,32},{128,64},{160,96},{192,128},{224,1... | collective-permute-start | bytes 196616 | tf_op jit(solution)/shard_map/ppermute | solution.py:157
  85.3 1.8 %collective-permute-done.28.rest_1_ = bf16[64,512]{1,0:T(8,128)(2,1)S(1)} collective-permute-done((bf16[64,512]{1,0:T(8,128)(2,1)S(1)}, bf16[64,512]{1,0:T(8,128)(2,1)S(1)}, u32[]{:S(2)}, u32[]{:S(2)}) %collective-permute-start.28) | collective-permute-done | bytes 65568 | tf_op jit(solution)/shard_map/ppermute | solution.py:157
  87.1 0.5 collective-permute-done.29.rest_2_
  87.6 0.9 shard_map.77
  88.5 7.3 %all-to-all-start = ((f32[32,8,128]{2,1,0:T(8,128)}), f32[32,8,128]{2,1,0:T(8,128)S(1)}, u32[]{:S(2)}, u32[]{:S(2)}) async-start(f32[32,8,128]{2,1,0:T(8,128)} %shard_map.77), calls=%async_computation | async-start | bytes 262144 | tf_op jit(solution)/shard_map/all_to_all | solution.py:269
  95.8 0.1 shard_map.74
  95.9 0.1 collective-permute-start.23
  95.9 3.2 %collective-permute-start.24 = (bf16[64,848]{1,0:T(8,128)(2,1)S(1)}, bf16[64,848]{1,0:T(8,128)(2,1)S(1)}, u32[]{:S(2)}, u32[]{:S(2)}) collective-permute-start(bf16[64,848]{1,0:T(8,128)(2,1)S(1)} %get-tuple-element.24), channel_id=1, source_target_pairs={{0,128},{32,160},{64,192},{96,224},{128,0},{160,32},{192,64},{224,... | collective-permute-start | bytes 325640 | tf_op jit(solution)/shard_map/ppermute | solution.py:157
  99.1 0.4 collective-permute-start.25
  99.5 1.3 %collective-permute-done.23.rest_0_ = bf16[64,848]{1,0:T(8,128)(2,1)S(1)} collective-permute-done((bf16[64,848]{1,0:T(8,128)(2,1)S(1)}, bf16[64,848]{1,0:T(8,128)(2,1)S(1)}, u32[]{:S(2)}, u32[]{:S(2)}) %collective-permute-start.23) | collective-permute-done | bytes 108576 | tf_op jit(solution)/shard_map/ppermute | solution.py:157
  100.8 1.8 %collective-permute-done.24.rest_1_ = bf16[64,848]{1,0:T(8,128)(2,1)S(1)} collective-permute-done((bf16[64,848]{1,0:T(8,128)(2,1)S(1)}, bf16[64,848]{1,0:T(8,128)(2,1)S(1)}, u32[]{:S(2)}, u32[]{:S(2)}) %collective-permute-start.24) | collective-permute-done | bytes 108576 | tf_op jit(solution)/shard_map/ppermute | solution.py:157
  102.6 0.5 collective-permute-done.25.rest_2_
  103.0 0.7 shard_map.75
  103.7 1.2 %all-to-all-done.pieces_ref = f32[32,8,128]{2,1,0:T(8,128)S(1)} async-done(((f32[32,8,128]{2,1,0:T(8,128)}), f32[32,8,128]{2,1,0:T(8,128)S(1)}, u32[]{:S(2)}, u32[]{:S(2)}) %all-to-all-start) | async-done | bytes 131104 | tf_op jit(solution)/shard_map/all_to_all | solution.py:269
  104.9 0.7 shard_map.78
  (31 shorter events, 0.2 us)
Async XLA Ops:
  0.6 60.1 %copy-start = (bf16[848,512]{1,0:T(8,128)(2,1)S(1)}, bf16[848,512]{1,0:T(8,128)(2,1)}, u32[]{:S(2)}) copy-start(bf16[848,512]{1,0:T(8,128)(2,1)} %features_ref.3) | copy-start | bytes 2605060
  2.5 5.7 %collective-permute-start = (bf16[106,256]{1,0:T(8,128)(2,1)S(1)}, bf16[106,256]{1,0:T(8,128)(2,1)S(1)}, u32[]{:S(2)}, u32[]{:S(2)}) collective-permute-start(bf16[106,256]{1,0:T(8,128)(2,1)S(1)} %get-tuple-element.33.refs_0_), channel_id=1, source_target_pairs={{0,8},{8,16},{16,24},{24,0},{1,9},{9,17},{17,25},{25,1},{2,10},{10... | collective-permute-start | bytes 162824 | tf_op jit(solution)/shard_map/ppermute | solution.py:25
  4.6 4.7 %collective-permute-start.1 = (bf16[106,256]{1,0:T(8,128)(2,1)S(1)}, bf16[106,256]{1,0:T(8,128)(2,1)S(1)}, u32[]{:S(2)}, u32[]{:S(2)}) collective-permute-start(bf16[106,256]{1,0:T(8,128)(2,1)S(1)} %get-tuple-element.33.refs_0_), channel_id=1, source_target_pairs={{0,16},{8,24},{16,0},{24,8},{1,17},{9,25},{17,1},{25,9},{2,18},{10... | collective-permute-start | bytes 162824 | tf_op jit(solution)/shard_map/ppermute | solution.py:25
  7.1 3.3 %collective-permute-start.2 = (bf16[106,256]{1,0:T(8,128)(2,1)S(1)}, bf16[106,256]{1,0:T(8,128)(2,1)S(1)}, u32[]{:S(2)}, u32[]{:S(2)}) collective-permute-start(bf16[106,256]{1,0:T(8,128)(2,1)S(1)} %get-tuple-element.33.refs_0_), channel_id=1, source_target_pairs={{0,24},{8,0},{16,8},{24,16},{1,25},{9,1},{17,9},{25,17},{2,26},{10... | collective-permute-start | bytes 162824 | tf_op jit(solution)/shard_map/ppermute | solution.py:25
  10.4 26.3 %collective-permute-start.3 = (bf16[4,106,256]{2,1,0:T(8,128)(2,1)S(1)}, bf16[4,106,256]{2,1,0:T(8,128)(2,1)S(1)}, u32[]{:S(2)}, u32[]{:S(2)}) collective-permute-start(bf16[4,106,256]{2,1,0:T(8,128)(2,1)S(1)} %shard_map.69.rest_0_), channel_id=1, source_target_pairs={{0,1},{1,2},{2,3},{3,4},{4,5},{5,6},{6,7},{7,0},{8,9},{9,10},{10,1... | collective-permute-start | bytes 651272 | tf_op jit(solution)/shard_map/ppermute | solution.py:25
  12.3 25.2 %collective-permute-start.4 = (bf16[4,106,256]{2,1,0:T(8,128)(2,1)S(1)}, bf16[4,106,256]{2,1,0:T(8,128)(2,1)S(1)}, u32[]{:S(2)}, u32[]{:S(2)}) collective-permute-start(bf16[4,106,256]{2,1,0:T(8,128)(2,1)S(1)} %shard_map.69.rest_0_), channel_id=1, source_target_pairs={{0,7},{1,0},{2,1},{3,2},{4,3},{5,4},{6,5},{7,6},{8,15},{9,8},{10,9... | collective-permute-start | bytes 651272 | tf_op jit(solution)/shard_map/ppermute | solution.py:25
  16.3 5.2 %collective-permute-start.11 = (bf16[106,256]{1,0:T(8,128)(2,1)S(1)}, bf16[106,256]{1,0:T(8,128)(2,1)S(1)}, u32[]{:S(2)}, u32[]{:S(2)}) collective-permute-start(bf16[106,256]{1,0:T(8,128)(2,1)S(1)} %get-tuple-element.32.refs_0_), channel_id=1, source_target_pairs={{0,1},{1,2},{2,3},{3,4},{4,5},{5,6},{6,7},{7,0},{8,9},{9,10},{10,1... | collective-permute-start | bytes 162824 | tf_op jit(solution)/shard_map/ppermute | solution.py:25
  16.3 9.4 %collective-permute-start.12 = (bf16[106,256]{1,0:T(8,128)(2,1)S(1)}, bf16[106,256]{1,0:T(8,128)(2,1)S(1)}, u32[]{:S(2)}, u32[]{:S(2)}) collective-permute-start(bf16[106,256]{1,0:T(8,128)(2,1)S(1)} %get-tuple-element.32.refs_0_), channel_id=1, source_target_pairs={{0,2},{1,3},{2,4},{3,5},{4,6},{5,7},{6,0},{7,1},{8,10},{9,11},{10,... | collective-permute-start | bytes 162824 | tf_op jit(solution)/shard_map/ppermute | solution.py:25
  18.1 9.3 %collective-permute-start.13 = (bf16[106,256]{1,0:T(8,128)(2,1)S(1)}, bf16[106,256]{1,0:T(8,128)(2,1)S(1)}, u32[]{:S(2)}, u32[]{:S(2)}) collective-permute-start(bf16[106,256]{1,0:T(8,128)(2,1)S(1)} %get-tuple-element.32.refs_0_), channel_id=1, source_target_pairs={{0,3},{1,4},{2,5},{3,6},{4,7},{5,0},{6,1},{7,2},{8,11},{9,12},{10,... | collective-permute-start | bytes 162824 | tf_op jit(solution)/shard_map/ppermute | solution.py:25
  21.5 8.7 %collective-permute-start.14 = (bf16[106,256]{1,0:T(8,128)(2,1)S(1)}, bf16[106,256]{1,0:T(8,128)(2,1)S(1)}, u32[]{:S(2)}, u32[]{:S(2)}) collective-permute-start(bf16[106,256]{1,0:T(8,128)(2,1)S(1)} %get-tuple-element.32.refs_0_), channel_id=1, source_target_pairs={{0,4},{1,5},{2,6},{3,7},{4,0},{5,1},{6,2},{7,3},{8,12},{9,13},{10,... | collective-permute-start | bytes 162824 | tf_op jit(solution)/shard_map/ppermute | solution.py:25
  25.7 5.7 %collective-permute-start.15 = (bf16[106,256]{1,0:T(8,128)(2,1)S(1)}, bf16[106,256]{1,0:T(8,128)(2,1)S(1)}, u32[]{:S(2)}, u32[]{:S(2)}) collective-permute-start(bf16[106,256]{1,0:T(8,128)(2,1)S(1)} %get-tuple-element.32.refs_0_), channel_id=1, source_target_pairs={{0,5},{1,6},{2,7},{3,0},{4,1},{5,2},{6,3},{7,4},{8,13},{9,14},{10,... | collective-permute-start | bytes 162824 | tf_op jit(solution)/shard_map/ppermute | solution.py:25
  27.4 5.1 %collective-permute-start.16 = (bf16[106,256]{1,0:T(8,128)(2,1)S(1)}, bf16[106,256]{1,0:T(8,128)(2,1)S(1)}, u32[]{:S(2)}, u32[]{:S(2)}) collective-permute-start(bf16[106,256]{1,0:T(8,128)(2,1)S(1)} %get-tuple-element.32.refs_0_), channel_id=1, source_target_pairs={{0,6},{1,7},{2,0},{3,1},{4,2},{5,3},{6,4},{7,5},{8,14},{9,15},{10,... | collective-permute-start | bytes 162824 | tf_op jit(solution)/shard_map/ppermute | solution.py:25
  30.2 3.8 %collective-permute-start.17 = (bf16[106,256]{1,0:T(8,128)(2,1)S(1)}, bf16[106,256]{1,0:T(8,128)(2,1)S(1)}, u32[]{:S(2)}, u32[]{:S(2)}) collective-permute-start(bf16[106,256]{1,0:T(8,128)(2,1)S(1)} %get-tuple-element.32.refs_0_), channel_id=1, source_target_pairs={{0,7},{1,0},{2,1},{3,2},{4,3},{5,4},{6,5},{7,6},{8,15},{9,8},{10,9... | collective-permute-start | bytes 162824 | tf_op jit(solution)/shard_map/ppermute | solution.py:25
  34.0 18.3 %collective-permute-start.18 = (bf16[8,106,256]{2,1,0:T(8,128)(2,1)S(1)}, bf16[8,106,256]{2,1,0:T(8,128)(2,1)S(1)}, u32[]{:S(2)}, u32[]{:S(2)}) collective-permute-start(bf16[8,106,256]{2,1,0:T(8,128)(2,1)S(1)} %shard_map.71.rest_0_), channel_id=1, source_target_pairs={{0,8},{8,16},{16,24},{24,0},{1,9},{9,17},{17,25},{25,1},{2,10},{10... | collective-permute-start | bytes 1302536 | tf_op jit(solution)/shard_map/ppermute | solution.py:25
  34.1 18.3 %collective-permute-start.19 = (bf16[8,106,256]{2,1,0:T(8,128)(2,1)S(1)}, bf16[8,106,256]{2,1,0:T(8,128)(2,1)S(1)}, u32[]{:S(2)}, u32[]{:S(2)}) collective-permute-start(bf16[8,106,256]{2,1,0:T(8,128)(2,1)S(1)} %shard_map.71.rest_0_), channel_id=1, source_target_pairs={{0,24},{8,0},{16,8},{24,16},{1,25},{9,1},{17,9},{25,17},{2,26},{10... | collective-permute-start | bytes 1302536 | tf_op jit(solution)/shard_map/ppermute | solution.py:25
  36.7 6.2 %collective-permute-start.5 = (bf16[4,106,256]{2,1,0:T(8,128)(2,1)S(1)}, bf16[4,106,256]{2,1,0:T(8,128)(2,1)}, u32[]{:S(2)}, u32[]{:S(2)}) collective-permute-start(bf16[4,106,256]{2,1,0:T(8,128)(2,1)S(1)} %collective-permute-done.3.rest_1_), channel_id=1, source_target_pairs={{0,1},{1,2},{2,3},{3,4},{4,5},{5,6},{6,7},{7,0},{8,9},{9,10},{10,1... | collective-permute-start | bytes 651272 | tf_op jit(solution)/shard_map/ppermute | solution.py:25
  36.8 0.7 copy-start.1
  37.5 5.6 %collective-permute-start.6 = (bf16[4,106,256]{2,1,0:T(8,128)(2,1)S(1)}, bf16[4,106,256]{2,1,0:T(8,128)(2,1)}, u32[]{:S(2)}, u32[]{:S(2)}) collective-permute-start(bf16[4,106,256]{2,1,0:T(8,128)(2,1)S(1)} %collective-permute-done.4.rest_2_), channel_id=1, source_target_pairs={{0,7},{1,0},{2,1},{3,2},{4,3},{5,4},{6,5},{7,6},{8,15},{9,8},{10,9... | collective-permute-start | bytes 651272 | tf_op jit(solution)/shard_map/ppermute | solution.py:25
  40.1 0.7 copy-start.3
  42.9 12.2 %collective-permute-start.7 = (bf16[4,106,256]{2,1,0:T(8,128)(2,1)}, bf16[4,106,256]{2,1,0:T(8,128)(2,1)S(1)}, u32[]{:S(2)}, u32[]{:S(2)}) collective-permute-start(bf16[4,106,256]{2,1,0:T(8,128)(2,1)} %collective-permute-done.5.rest_3_), channel_id=1, source_target_pairs={{0,1},{1,2},{2,3},{3,4},{4,5},{5,6},{6,7},{7,0},{8,9},{9,10},{10,1... | collective-permute-start | bytes 651272 | tf_op jit(solution)/shard_map/ppermute | solution.py:25
  43.1 12.2 %collective-permute-start.8 = (bf16[4,106,256]{2,1,0:T(8,128)(2,1)}, bf16[4,106,256]{2,1,0:T(8,128)(2,1)S(1)}, u32[]{:S(2)}, u32[]{:S(2)}) collective-permute-start(bf16[4,106,256]{2,1,0:T(8,128)(2,1)} %collective-permute-done.6.rest_4_), channel_id=1, source_target_pairs={{0,7},{1,0},{2,1},{3,2},{4,3},{5,4},{6,5},{7,6},{8,15},{9,8},{10,9... | collective-permute-start | bytes 651272 | tf_op jit(solution)/shard_map/ppermute | solution.py:25
  47.3 13.5 %copy-start.2 = (bf16[4,106,256]{2,1,0:T(8,128)(2,1)S(1)}, bf16[4,106,256]{2,1,0:T(8,128)(2,1)}, u32[]{:S(2)}) copy-start(bf16[4,106,256]{2,1,0:T(8,128)(2,1)} %copy-done.1) | copy-start | bytes 651268
  47.3 13.4 %copy-start.4 = (bf16[4,106,256]{2,1,0:T(8,128)(2,1)S(1)}, bf16[4,106,256]{2,1,0:T(8,128)(2,1)}, u32[]{:S(2)}) copy-start(bf16[4,106,256]{2,1,0:T(8,128)(2,1)} %copy-done.3) | copy-start | bytes 651268
  52.2 26.7 %copy-start.5 = (bf16[512,512]{1,0:T(8,128)(2,1)S(1)}, bf16[512,512]{1,0:T(8,128)(2,1)}, u32[]{:S(2)}) copy-start(bf16[512,512]{1,0:T(8,128)(2,1)} %weight_ref.1) | copy-start | bytes 1572868
  52.3 12.2 %collective-permute-start.20 = (bf16[4,106,256]{2,1,0:T(8,128)(2,1)S(1)}, bf16[4,106,256]{2,1,0:T(8,128)(2,1)S(1)}, u32[]{:S(2)}, u32[]{:S(2)}) collective-permute-start(bf16[4,106,256]{2,1,0:T(8,128)(2,1)S(1)} %slice.28), channel_id=1, source_target_pairs={{0,8},{8,16},{16,24},{24,0},{1,9},{9,17},{17,25},{25,1},{2,10},{10... | collective-permute-start | bytes 651272 | tf_op jit(solution)/shard_map/ppermute | solution.py:25
  52.4 12.1 %collective-permute-start.21 = (bf16[4,106,256]{2,1,0:T(8,128)(2,1)S(1)}, bf16[4,106,256]{2,1,0:T(8,128)(2,1)S(1)}, u32[]{:S(2)}, u32[]{:S(2)}) collective-permute-start(bf16[4,106,256]{2,1,0:T(8,128)(2,1)S(1)} %slice.29), channel_id=1, source_target_pairs={{0,24},{8,0},{16,8},{24,16},{1,25},{9,1},{17,9},{25,17},{2,26},{10... | collective-permute-start | bytes 651272 | tf_op jit(solution)/shard_map/ppermute | solution.py:25
  55.2 5.3 %collective-permute-start.9 = (bf16[2,106,256]{2,1,0:T(8,128)(2,1)S(1)}, bf16[2,106,256]{2,1,0:T(8,128)(2,1)S(1)}, u32[]{:S(2)}, u32[]{:S(2)}) collective-permute-start(bf16[2,106,256]{2,1,0:T(8,128)(2,1)S(1)} %slice.25), channel_id=1, source_target_pairs={{0,1},{1,2},{2,3},{3,4},{4,5},{5,6},{6,7},{7,0},{8,9},{9,10},{10,1... | collective-permute-start | bytes 325640 | tf_op jit(solution)/shard_map/ppermute | solution.py:25
  55.3 5.4 %collective-permute-start.10 = (bf16[2,106,256]{2,1,0:T(8,128)(2,1)S(1)}, bf16[2,106,256]{2,1,0:T(8,128)(2,1)S(1)}, u32[]{:S(2)}, u32[]{:S(2)}) collective-permute-start(bf16[2,106,256]{2,1,0:T(8,128)(2,1)S(1)} %slice.26), channel_id=1, source_target_pairs={{0,7},{1,0},{2,1},{3,2},{4,3},{5,4},{6,5},{7,6},{8,15},{9,8},{10,9... | collective-permute-start | bytes 325640 | tf_op jit(solution)/shard_map/ppermute | solution.py:25
  68.0 12.2 %collective-permute-start.26 = (bf16[4,64,512]{2,1,0:T(8,128)(2,1)S(1)}, bf16[4,64,512]{2,1,0:T(8,128)(2,1)S(1)}, u32[]{:S(2)}, u32[]{:S(2)}) collective-permute-start(bf16[4,64,512]{2,1,0:T(8,128)(2,1)S(1)} %get-tuple-element.27), channel_id=1, source_target_pairs={{0,32},{32,0},{64,96},{96,64},{128,160},{160,128},{192,224},{224,1... | collective-permute-start | bytes 786440 | tf_op jit(solution)/shard_map/ppermute | solution.py:151
  79.8 15.9 %collective-permute-start.22 = (bf16[4,64,848]{2,1,0:T(8,128)(2,1)S(1)}, bf16[4,64,848]{2,1,0:T(8,128)(2,1)S(1)}, u32[]{:S(2)}, u32[]{:S(2)}) collective-permute-start(bf16[4,64,848]{2,1,0:T(8,128)(2,1)S(1)} %get-tuple-element.21), channel_id=1, source_target_pairs={{0,32},{32,0},{64,96},{96,64},{128,160},{160,128},{192,224},{224,1... | collective-permute-start | bytes 1302536 | tf_op jit(solution)/shard_map/ppermute | solution.py:151
  80.2 5.1 %collective-permute-start.27 = (bf16[64,512]{1,0:T(8,128)(2,1)S(1)}, bf16[64,512]{1,0:T(8,128)(2,1)S(1)}, u32[]{:S(2)}, u32[]{:S(2)}) collective-permute-start(bf16[64,512]{1,0:T(8,128)(2,1)S(1)} %get-tuple-element.29), channel_id=1, source_target_pairs={{0,64},{32,96},{64,128},{96,160},{128,192},{160,224},{192,0},{224,... | collective-permute-start | bytes 196616 | tf_op jit(solution)/shard_map/ppermute | solution.py:157
  81.6 5.5 %collective-permute-start.28 = (bf16[64,512]{1,0:T(8,128)(2,1)S(1)}, bf16[64,512]{1,0:T(8,128)(2,1)S(1)}, u32[]{:S(2)}, u32[]{:S(2)}) collective-permute-start(bf16[64,512]{1,0:T(8,128)(2,1)S(1)} %get-tuple-element.30), channel_id=1, source_target_pairs={{0,128},{32,160},{64,192},{96,224},{128,0},{160,32},{192,64},{224,... | collective-permute-start | bytes 196616 | tf_op jit(solution)/shard_map/ppermute | solution.py:157
  84.2 3.4 %collective-permute-start.29 = (bf16[64,512]{1,0:T(8,128)(2,1)S(1)}, bf16[64,512]{1,0:T(8,128)(2,1)S(1)}, u32[]{:S(2)}, u32[]{:S(2)}) collective-permute-start(bf16[64,512]{1,0:T(8,128)(2,1)S(1)} %get-tuple-element.31), channel_id=1, source_target_pairs={{0,192},{32,224},{64,0},{96,32},{128,64},{160,96},{192,128},{224,1... | collective-permute-start | bytes 196616 | tf_op jit(solution)/shard_map/ppermute | solution.py:157
  88.5 16.4 %all-to-all-start = ((f32[32,8,128]{2,1,0:T(8,128)}), f32[32,8,128]{2,1,0:T(8,128)S(1)}, u32[]{:S(2)}, u32[]{:S(2)}) async-start(f32[32,8,128]{2,1,0:T(8,128)} %shard_map.77), calls=%async_computation | async-start | bytes 262144 | tf_op jit(solution)/shard_map/all_to_all | solution.py:269
  95.9 4.9 %collective-permute-start.23 = (bf16[64,848]{1,0:T(8,128)(2,1)S(1)}, bf16[64,848]{1,0:T(8,128)(2,1)S(1)}, u32[]{:S(2)}, u32[]{:S(2)}) collective-permute-start(bf16[64,848]{1,0:T(8,128)(2,1)S(1)} %get-tuple-element.23), channel_id=1, source_target_pairs={{0,64},{32,96},{64,128},{96,160},{128,192},{160,224},{192,0},{224,... | collective-permute-start | bytes 325640 | tf_op jit(solution)/shard_map/ppermute | solution.py:157
  95.9 6.6 %collective-permute-start.24 = (bf16[64,848]{1,0:T(8,128)(2,1)S(1)}, bf16[64,848]{1,0:T(8,128)(2,1)S(1)}, u32[]{:S(2)}, u32[]{:S(2)}) collective-permute-start(bf16[64,848]{1,0:T(8,128)(2,1)S(1)} %get-tuple-element.24), channel_id=1, source_target_pairs={{0,128},{32,160},{64,192},{96,224},{128,0},{160,32},{192,64},{224,... | collective-permute-start | bytes 325640 | tf_op jit(solution)/shard_map/ppermute | solution.py:157
  99.1 3.9 %collective-permute-start.25 = (bf16[64,848]{1,0:T(8,128)(2,1)S(1)}, bf16[64,848]{1,0:T(8,128)(2,1)S(1)}, u32[]{:S(2)}, u32[]{:S(2)}) collective-permute-start(bf16[64,848]{1,0:T(8,128)(2,1)S(1)} %get-tuple-element.25), channel_id=1, source_target_pairs={{0,192},{32,224},{64,0},{96,32},{128,64},{160,96},{192,128},{224,1... | collective-permute-start | bytes 325640 | tf_op jit(solution)/shard_map/ppermute | solution.py:157

commit v2 on v1

--- a/solution.py
+++ b/solution.py
@@ -15,6 +15,7 @@
 NT = (((1,), (1,)), ((), ()))
 TN = (((0,), (0,)), ((), ()))
 CORES = 2
+LANES = 128
 
 VMEM = pl.BlockSpec(memory_space=pltpu.VMEM)
 SMEM = pl.BlockSpec(memory_space=pltpu.SMEM)
@@ -25,54 +26,97 @@
     return lax.ppermute(value, axis, [(i, (i + step) % n) for i in range(n)])
 
 
-def call(body, out, args, scratch=(), smem=1, flops=1 << 20, limit=16):
+def call(body, out, args, scratch=(), smem=1, flops=1 << 20, limit=16, aliases=()):
     return pl.pallas_call(
         body,
         out_shape=out,
         in_specs=[SMEM] * smem + [VMEM] * (len(args) - smem),
         out_specs=jax.tree.map(lambda _: VMEM, out),
         scratch_shapes=list(scratch),
+        input_output_aliases=dict(aliases),
         compiler_params=pltpu.CompilerParams(vmem_limit_bytes=limit << 20),
         cost_estimate=pl.CostEstimate(flops=flops, bytes_accessed=1 << 20, transcendentals=0),
     )(*args)
 
 
-def arrange_kernel(steps, me_ref, *refs):
-    *pieces, out_ref = refs
-    n = out_ref.shape[0]
-    for step, ref in zip(steps, pieces):
-        out_ref[lax.rem(me_ref[0] + (step + n), n)] = ref[...]
-
-
-def convert_kernel(tile_ref, out_ref):
-    out_ref[...] = tile_ref[...].astype(jnp.float32).astype(jnp.bfloat16)
-
-
-def product(x_major, me_ref, tile_ref, scale_ref, refs, slots, rows):
-    n, m, length, _ = slots.shape
-    me = me_ref[0]
-    own, _, _ = refs[:3]
-    slots[me] = own[...]
-    for step in range(1, n // 2):
-        up, down = refs[2 * step - 1], refs[2 * step]
-        slots[lax.rem(me + (n - step), n)] = up[...]
-        slots[lax.rem(me + step, n)] = down[...]
-    across = lax.rem(me + n // 2, n)
-    slots[across, : m // 2] = refs[-2][...]
-    slots[across, m // 2 :] = refs[-1][...]
-    for i in range(n):
-        for j in range(m):
-            k = i * m + j if x_major else j * n + i
-            rows[pl.ds(k * length, length), :] = slots[i, j].astype(jnp.float32)
-    total = jnp.dot(
-        tile_ref[...], rows[...].astype(jnp.bfloat16), preferred_element_type=jnp.float32
-    )
-    return (total * scale_ref[...]).astype(jnp.bfloat16)
-
-
-def first_kernel(me_ref, tile_ref, scale_ref, features_ref, *rest):
-    *refs, out_ref, r_ref, slots, rows = rest
-    out_ref[...] = product(False, me_ref, tile_ref, scale_ref, refs, slots, rows)
+def arrange_kernel(me_ref, *refs):
+    *pieces, out_0, out_1 = refs
+    n, (length, half) = len(pieces), (pieces[0].shape[0], out_0.shape[1])
+    for me in range(n):
+
+        @pl.when(me_ref[0] == me)
+        def _():
+            for step, ref in enumerate(pieces):
+                here = pl.ds((me - step) % n * length, length)
+                out_0[here, :] = ref[:, :half]
+                out_1[here, :] = ref[:, half:]
+
+
+def cut_kernel(start, value_ref, out_ref):
+    out_ref[...] = value_ref[pl.ds(start, out_ref.shape[0]), :]
+
+
+def convert_kernel(start, tile_hbm, out_ref, held, sems):
+    step = 16
+    parts = sems.shape[0]
+    groups = held.shape[0] // step
+    bounds = [groups * k // parts for k in range(parts + 1)]
+
+    def copy(k):
+        here, size = bounds[k] * step, (bounds[k + 1] - bounds[k]) * step
+        return pltpu.make_async_copy(
+            tile_hbm.at[pl.ds(start + here, size), :], held.at[pl.ds(here, size), :], sems.at[k]
+        )
+
+    for k in range(parts):
+        copy(k).start()
+    for k in range(parts):
+        copy(k).wait()
+
+        @pl.loop(bounds[k], bounds[k + 1])
+        def _(i):
+            here = pl.ds(pl.multiple_of(i * step, step), step)
+            out_ref[here, :] = held[here, :].astype(jnp.float32).astype(jnp.bfloat16)
+
+
+def lay(me, n_x, n_z, units, rows_refs):
+    for step, parts in units:
+        z = lax.rem(me + (n_z + step), n_z)
+        length = sum(ref.shape[0] for ref in parts) // n_x
+        first = 0
+        for ref in parts:
+            last = first + ref.shape[0]
+            for x in range(n_x):
+                a, b = max(first, x * length), min(last, (x + 1) * length)
+                if a < b:
+                    here = pl.ds((x * n_z + z) * length + (a - x * length), b - a)
+                    for c, rows_ref in enumerate(rows_refs):
+                        rows_ref[here, :] = ref[
+                            a - first : b - first, c * LANES : (c + 1) * LANES
+                        ].astype(jnp.float32)
+            first = last
+
+
+def early_kernel(n_x, n_z, me_ref, *rest):
+    *units, rows_0, rows_1 = rest
+    steps = [0] + [s * k for k in range(1, n_z // 2) for s in (-1, 1)]
+    lay(me_ref[0], n_x, n_z, [(s, [ref]) for s, ref in zip(steps, units)], (rows_0, rows_1))
+
+
+def late(n_x, n_z, me, tile_refs, scale_ref, up, down, rows_refs, out_ref):
+    lay(me, n_x, n_z, [(n_z // 2, [up, down])], rows_refs)
+    rows = jnp.concatenate([ref[...].astype(jnp.bfloat16) for ref in rows_refs], axis=1)
+    first = 0
+    for tile_ref in tile_refs:
+        here = pl.ds(first, tile_ref.shape[0])
+        total = jnp.dot(tile_ref[...], rows, preferred_element_type=jnp.float32)
+        out_ref[here, :] = (total * scale_ref[here, :]).astype(jnp.bfloat16)
+        first += tile_ref.shape[0]
+
+
+def first_kernel(n_x, n_z, me_ref, tile_0, tile_1, scale_ref, features_ref, *rest):
+    up, down, _, _, out_ref, r_ref, *rows_refs = rest
+    late(n_x, n_z, me_ref[0], (tile_0, tile_1), scale_ref, up, down, rows_refs, out_ref)
     r_ref[...] = lax.dot_general(
         out_ref[...], features_ref[...], TN, preferred_element_type=jnp.float32
     )
@@ -84,16 +128,18 @@
         send_ref[y] = held[CORES * y + (CORES - 1 - core)].astype(send_ref.dtype)
 
 
-def second_kernel(me_ref, tile_ref, scale_ref, features_ref, r_first_ref, *rest):
-    *refs, out_ref, keep_ref, send_ref, slots, rows, held = rest
-    out_ref[...] = product(True, me_ref, tile_ref, scale_ref, refs, slots, rows)
+def second_kernel(
+    n_x, n_z, me_ref, core_ref, tile_0, tile_1, scale_ref, features_ref, r_first_ref, *rest
+):
+    up, down, _, _, out_ref, keep_ref, send_ref, *rows_refs, held = rest
+    late(n_x, n_z, me_ref[0], (tile_0, tile_1), scale_ref, up, down, rows_refs, out_ref)
     r = lax.dot_general(
         out_ref[...], features_ref[...], TN, preferred_element_type=jnp.float32
     )
     n_row, share, width = held.shape
     held[: n_row // 2] = r_first_ref[...].reshape(n_row // 2, share, width)
     held[n_row // 2 :] = r.reshape(n_row // 2, share, width)
-    parted(me_ref[1], held, keep_ref, send_ref)
+    parted(core_ref[0], held, keep_ref, send_ref)
 
 
 def q_kernel(me_ref, first_ref, second_ref, weight_ref, keep_ref, send_ref, held):
@@ -170,80 +216,105 @@
     n_row = lax.axis_size("row")
     n_y = n_row // CORES
     col = lax.axis_index(COL)
-    y, core = row // CORES, row % CORES
+    y, core = lax.div(row, CORES), lax.rem(row, CORES)
+
+    row_start = (row * rows_here + col * length).astype(jnp.uint32)
+    col_start = (col * cols_here).astype(jnp.uint32)
+    cotangent, x, z, y, core, row_start, col_start = lax.optimization_barrier(
+        (cotangent, x, z, y, core, row_start, col_start)
+    )
 
     def inv_root(start, size):
-        return lax.rsqrt(lax.dynamic_slice_in_dim(degree, start, size, 0).astype(jnp.float32))
+        return lax.rsqrt(lax.dynamic_slice(degree, (start,), (size,)).astype(jnp.float32))
 
     scaled = (
         cotangent.astype(jnp.float32)
-        * inv_root(row * rows_here + col * length, length)[:, None]
+        * inv_root(row_start, length)[:, None]
     ).astype(jnp.bfloat16)
-    mine_a, mine_b = scaled[:, :half], scaled[:, half:]
-    tile = call(
-        convert_kernel,
-        jax.ShapeDtypeStruct((cols_here, rows_here), jnp.bfloat16),
-        (adjacency.T,),
-        smem=0,
-        limit=40,
-    )
-    col_scale = inv_root(col * cols_here, cols_here)[:, None]
+    col_scale = inv_root(col_start, cols_here)[:, None]
+
+    def converted(start, size):
+        return pl.pallas_call(
+            functools.partial(convert_kernel, start),
+            out_shape=jax.ShapeDtypeStruct((size, rows_here), jnp.bfloat16),
+            in_specs=[pl.BlockSpec(memory_space=pltpu.HBM)],
+            out_specs=VMEM,
+            scratch_shapes=[
+                pltpu.VMEM((size, rows_here), jnp.int32),
+                pltpu.SemaphoreType.DMA((4,)),
+            ],
+            compiler_params=pltpu.CompilerParams(vmem_limit_bytes=46 << 20),
+            cost_estimate=pl.CostEstimate(flops=1 << 24, bytes_accessed=9 << 20, transcendentals=0),
+            name="convert",
+        )(adjacency.T)
+
+    split = cols_here // 32 * 16
+    tiles = (converted(0, split), converted(split, cols_here - split))
 
     unit = functools.partial(jax.ShapeDtypeStruct, dtype=jnp.bfloat16)
-    near = [shifted(mine_a, X, s) for s in range(1, nx)]
-    a = call(
-        functools.partial(arrange_kernel, [0] + [-s for s in range(1, nx)]),
-        unit((nx, length, half)),
-        (x.reshape(1), mine_a, *near),
-    )
-    far = [shifted(mine_b, Z, s) for s in range(1, nz)]
-    b = call(
-        functools.partial(arrange_kernel, [0] + [-s for s in range(1, nz)]),
-        unit((nz, length, half)),
-        (z.reshape(1), mine_b, *far),
-    )
-
-    def ring(own, axis):
-        n = lax.axis_size(axis)
-        middle = own.shape[0] // 2
+
+    near = [shifted(scaled, X, s) for s in range(1, nx)]
+    run = nx * length
+    middle = run // 2 // 16 * 16
+    a, b = call(
+        arrange_kernel, (unit((run, half)), unit((run, half))), (x.reshape(1), scaled, *near)
+    )
+
+    def cut(value, start, stop):
+        return call(
+            functools.partial(cut_kernel, start), unit((stop - start, half)), (value,), smem=0
+        )
+
+    def ring(own):
         units, up, down = [own], own, own
-        for step in range(1, n // 2 + 1):
-            if step == n // 2:
-                up, down = up[:middle], down[middle:]
-            up = shifted(up, axis, 1)
-            down = shifted(down, axis, -1)
+        for step in range(1, nz // 2 + 1):
+            if step == nz // 2:
+                up, down = cut(up, 0, middle), cut(down, middle, run)
+            up = shifted(up, Z, 1)
+            down = shifted(down, Z, -1)
             units += [up, down]
         return units
 
-    a_units = ring(a, Z)
-    b_units = ring(b, X)
+    column = jax.ShapeDtypeStruct((rows_here, LANES), jnp.float32)
+
+    def early(units):
+        return call(
+            functools.partial(early_kernel, nx, nz), (column, column), (z.reshape(1), *units)
+        )
 
     flops = 2 * rows_here * cols_here * half
-    rows_buffer = pltpu.VMEM((rows_here, half), jnp.float32)
-    first, r_first = call(
-        first_kernel,
-        (unit((cols_here, half)), jax.ShapeDtypeStruct((half, width), jnp.float32)),
-        (z.reshape(1), tile, col_scale, features, *a_units),
-        scratch=(pltpu.VMEM((nz, nx, length, half), jnp.bfloat16), rows_buffer),
+    a_units, b_units = ring(a), ring(b)
+    first, r_first, *_ = call(
+        functools.partial(first_kernel, nx, nz),
+        (unit((cols_here, half)), jax.ShapeDtypeStruct((half, width), jnp.float32), column, column),
+        (z.reshape(1), *tiles, col_scale, features, *a_units[7:], *early(a_units[:7])),
         flops=flops,
-        limit=32,
+        aliases={7: 2, 8: 3},
     )
     share = width // n_row
-    second, r_keep, r_send = call(
-        second_kernel,
+    second, r_keep, r_send, *_ = call(
+        functools.partial(second_kernel, nx, nz),
         (
             unit((cols_here, half)),
             jax.ShapeDtypeStruct((n_y, share, width), jnp.float32),
             unit((n_y, share, width)),
+            column,
+            column,
         ),
-        (jnp.stack([x, core]), tile, col_scale, features, r_first, *b_units),
-        scratch=(
-            pltpu.VMEM((nx, nz, length, half), jnp.bfloat16),
-            rows_buffer,
-            pltpu.VMEM((n_row, share, width), jnp.float32),
+        (
+            z.reshape(1),
+            core.reshape(1),
+            *tiles,
+            col_scale,
+            features,
+            r_first,
+            *b_units[7:],
+            *early(b_units[:7]),
         ),
+        scratch=(pltpu.VMEM((n_row, share, width), jnp.float32),),
+        smem=2,
         flops=flops,
-        limit=32,
+        aliases={9: 3, 10: 4},
     )
     q_keep, q_send = call(
         q_kernel,

time: 107 us -> 93 us (0.87)
  starting transfers between devices: 66.2 us -> 53.4 us
  Pallas kernels: 15.5 us -> 14 us
  waiting for transfers between devices: 18.7 us -> 20.2 us
  local copies, waits for them, and re-layouts: 1.63 us -> 0.18 us
    ppermute x22 -> x19, starting transfers between devices: 39.1 us -> 30.6 us  [shifted(): return lax.ppermute(value, axis, [(i, (i + step) % n) for i in range(n)])]
    pallas_call x11 -> x15, Pallas kernels: 15.5 us -> 8.33 us  [call(): pl.pallas_call(body, out_shape=out, in_specs=[SMEM] * smem + [VMEM] * (le...]
    pallas_call x0 -> x2, Pallas kernels: none -> 5.7 us  [converted(): pl.pallas_call(functools.partial(convert_kernel, start), out_shape=jax.Sh...]
    ppermute x2, starting transfers between devices: 11.1 us -> 5.61 us  [over_rows(): got = lax.ppermute(send, 'row', [(i, i ^ 1) for i in range(n)])]
    ppermute x22 -> x19, waiting for transfers between devices: 11.4 us -> 13 us  [shifted(): return lax.ppermute(value, axis, [(i, (i + step) % n) for i in range(n)])]
    unnamed x12 -> x4, local copies, waits for them, and re-layouts: 1.4 us -> 0.01 us
    all_to_all x1, starting transfers between devices: 7.26 us -> 8.4 us  [per_device(): lax.all_to_all(packed, COL, split_axis=0, concat_axis=0, tiled=True)]
  transfers between devices with their start and end apart: 31 -> 28, of which waited for: 17 -> 13; matrix products, arithmetic and copies ran while one was open for 1% -> 1% of each run, Pallas kernels for 11% -> 12%
where the time goes in v2:
time: 93 us; the launch traced here: 91.2 us
  starting transfers between devices  53.4 us (57%)
  waiting for transfers between devices  20.2 us (22%)
  Pallas kernels  14 us (15%)
  other arithmetic  2.53 us (3%)
    ppermute x19, starting transfers between devices, shifted(): return lax.ppermute(value, axis, [(i, (i + step) % n) for i in range(n)])  30.6 us
    ppermute x19, waiting for transfers between devices, shifted(): return lax.ppermute(value, axis, [(i, (i + step) % n) for i in range(n)])  13 us
    ppermute x6, starting transfers between devices, over_rows(): lax.ppermute(part, 'row', [(i, (i + CORES * step) % n) for i in range(n)])  8.7 us
    all_to_all x1, starting transfers between devices, per_device(): lax.all_to_all(packed, COL, split_axis=0, concat_axis=0, tiled=True)  8.4 us
    pallas_call x15, Pallas kernels, call(): pl.pallas_call(body, out_shape=out, in_specs=[SMEM] * smem + [VMEM] * (le...  8.33 us
    ppermute x6, waiting for transfers between devices, over_rows(): lax.ppermute(part, 'row', [(i, (i + CORES * step) % n) for i in range(n)])  5.89 us
    pallas_call x2, Pallas kernels, converted(): pl.pallas_call(functools.partial(convert_kernel, start), out_shape=jax.Sh...  5.7 us
    ppermute x2, starting transfers between devices, over_rows(): got = lax.ppermute(send, 'row', [(i, i ^ 1) for i in range(n)])  5.61 us
  transfers between devices with their start and end apart: 28, of which 13 were waited for; matrix products, arithmetic and copies ran while one was open for 1% of the time, Pallas kernels for 12%

profile of v2, /device:TPU:1, one launch (start us, length us, event | category | flops | bytes accessed | tf_op | source)
XLA Modules:
  0.0 91.2 jit_solution(18266812948951024527)
XLA Ops:
  0.6 0.8 convert_rsqrt_fusion.1
  1.4 1.0 %multiply_convert_fusion.refs_0_ = bf16[106,512]{1,0:T(8,128)(2,1)S(1)} fusion(bf16[106,512]{1,0:T(8,128)(2,1)} %param.7, f32[106]{0:T(128)S(1)} %convert_rsqrt_fusion.1), kind=kLoop, calls=%fused_computation | loop fusion | flops 162816 | bytes 217512 | tf_op jit(solution)/shard_map/convert_element_type | solution.py:233
  2.4 2.1 %collective-permute-start = (bf16[106,512]{1,0:T(8,128)(2,1)S(1)}, bf16[106,512]{1,0:T(8,128)(2,1)S(1)}, u32[]{:S(2)}, u32[]{:S(2)}) collective-permute-start(bf16[106,512]{1,0:T(8,128)(2,1)S(1)} %multiply_convert_fusion.refs_0_), channel_id=1, source_target_pairs={{0,8},{8,16},{16,24},{24,0},{1,9},{9,17},{17,25},{25,1},{2,10},{10... | collective-permute-start | bytes 325640 | tf_op jit(solution)/shard_map/ppermute | solution.py:26
  4.5 2.5 %collective-permute-start.1 = (bf16[106,512]{1,0:T(8,128)(2,1)S(1)}, bf16[106,512]{1,0:T(8,128)(2,1)S(1)}, u32[]{:S(2)}, u32[]{:S(2)}) collective-permute-start(bf16[106,512]{1,0:T(8,128)(2,1)S(1)} %multiply_convert_fusion.refs_0_), channel_id=1, source_target_pairs={{0,16},{8,24},{16,0},{24,8},{1,17},{9,25},{17,1},{25,9},{2,18},{10... | collective-permute-start | bytes 325640 | tf_op jit(solution)/shard_map/ppermute | solution.py:26
  7.0 1.2 %collective-permute-start.2 = (bf16[106,512]{1,0:T(8,128)(2,1)S(1)}, bf16[106,512]{1,0:T(8,128)(2,1)S(1)}, u32[]{:S(2)}, u32[]{:S(2)}) collective-permute-start(bf16[106,512]{1,0:T(8,128)(2,1)S(1)} %multiply_convert_fusion.refs_0_), channel_id=1, source_target_pairs={{0,24},{8,0},{16,8},{24,16},{1,25},{9,1},{17,9},{25,17},{2,26},{10... | collective-permute-start | bytes 325640 | tf_op jit(solution)/shard_map/ppermute | solution.py:26
  8.1 0.0 collective-permute-done.refs_1_
  8.1 3.9 %collective-permute-done.1.refs_2_ = bf16[106,512]{1,0:T(8,128)(2,1)S(1)} collective-permute-done((bf16[106,512]{1,0:T(8,128)(2,1)S(1)}, bf16[106,512]{1,0:T(8,128)(2,1)S(1)}, u32[]{:S(2)}, u32[]{:S(2)}) %collective-permute-start.1) | collective-permute-done | bytes 108576 | tf_op jit(solution)/shard_map/ppermute | solution.py:26
  12.0 0.1 shard_map.68
  12.1 1.7 %collective-permute-start.3 = (bf16[424,256]{1,0:T(8,128)(2,1)S(1)}, bf16[424,256]{1,0:T(8,128)(2,1)S(1)}, u32[]{:S(2)}, u32[]{:S(2)}) collective-permute-start(bf16[424,256]{1,0:T(8,128)(2,1)S(1)} %get-tuple-element.37.rest_0_), channel_id=1, source_target_pairs={{0,1},{1,2},{2,3},{3,4},{4,5},{5,6},{6,7},{7,0},{8,9},{9,10},{10,1... | collective-permute-start | bytes 651272 | tf_op jit(solution)/shard_map/ppermute | solution.py:26
  13.8 4.0 %collective-permute-start.7 = (bf16[424,256]{1,0:T(8,128)(2,1)S(1)}, bf16[424,256]{1,0:T(8,128)(2,1)S(1)}, u32[]{:S(2)}, u32[]{:S(2)}) collective-permute-start(bf16[424,256]{1,0:T(8,128)(2,1)S(1)} %get-tuple-element.37.rest_0_), channel_id=1, source_target_pairs={{0,7},{1,0},{2,1},{3,2},{4,3},{5,4},{6,5},{7,6},{8,15},{9,8},{10,9... | collective-permute-start | bytes 651272 | tf_op jit(solution)/shard_map/ppermute | solution.py:26
  17.8 0.0 collective-permute-start.11
  17.8 2.7 %collective-permute-start.15 = (bf16[424,256]{1,0:T(8,128)(2,1)S(1)}, bf16[424,256]{1,0:T(8,128)(2,1)S(1)}, u32[]{:S(2)}, u32[]{:S(2)}) collective-permute-start(bf16[424,256]{1,0:T(8,128)(2,1)S(1)} %get-tuple-element.42.rest_0_), channel_id=1, source_target_pairs={{0,7},{1,0},{2,1},{3,2},{4,3},{5,4},{6,5},{7,6},{8,15},{9,8},{10,9... | collective-permute-start | bytes 651272 | tf_op jit(solution)/shard_map/ppermute | solution.py:26
  20.5 1.4 %collective-permute-done.3.rest_1_ = bf16[424,256]{1,0:T(8,128)(2,1)S(1)} collective-permute-done((bf16[424,256]{1,0:T(8,128)(2,1)S(1)}, bf16[424,256]{1,0:T(8,128)(2,1)S(1)}, u32[]{:S(2)}, u32[]{:S(2)}) %collective-permute-start.3) | collective-permute-done | bytes 217120 | tf_op jit(solution)/shard_map/ppermute | solution.py:26
  21.9 0.0 collective-permute-start.4
  21.9 0.0 collective-permute-done.7.rest_2_
  21.9 2.7 %collective-permute-start.8 = (bf16[424,256]{1,0:T(8,128)(2,1)S(1)}, bf16[424,256]{1,0:T(8,128)(2,1)S(1)}, u32[]{:S(2)}, u32[]{:S(2)}) collective-permute-start(bf16[424,256]{1,0:T(8,128)(2,1)S(1)} %collective-permute-done.7.rest_2_), channel_id=1, source_target_pairs={{0,7},{1,0},{2,1},{3,2},{4,3},{5,4},{6,5},{7,6},{8,15},{9,8},{10,9... | collective-permute-start | bytes 651272 | tf_op jit(solution)/shard_map/ppermute | solution.py:26
  24.6 2.0 %collective-permute-done.11.rest_1_ = bf16[424,256]{1,0:T(8,128)(2,1)S(1)} collective-permute-done((bf16[424,256]{1,0:T(8,128)(2,1)S(1)}, bf16[424,256]{1,0:T(8,128)(2,1)S(1)}, u32[]{:S(2)}, u32[]{:S(2)}) %collective-permute-start.11) | collective-permute-done | bytes 217120 | tf_op jit(solution)/shard_map/ppermute | solution.py:26
  26.6 0.0 collective-permute-start.12
  26.6 2.7 %collective-permute-start.16 = (bf16[424,256]{1,0:T(8,128)(2,1)S(1)}, bf16[424,256]{1,0:T(8,128)(2,1)S(1)}, u32[]{:S(2)}, u32[]{:S(2)}) collective-permute-start(bf16[424,256]{1,0:T(8,128)(2,1)S(1)} %collective-permute-done.15.rest_2_), channel_id=1, source_target_pairs={{0,7},{1,0},{2,1},{3,2},{4,3},{5,4},{6,5},{7,6},{8,15},{9,8},{10,9... | collective-permute-start | bytes 651272 | tf_op jit(solution)/shard_map/ppermute | solution.py:26
  29.3 1.8 %collective-permute-done.4.rest_3_ = bf16[424,256]{1,0:T(8,128)(2,1)S(1)} collective-permute-done((bf16[424,256]{1,0:T(8,128)(2,1)S(1)}, bf16[424,256]{1,0:T(8,128)(2,1)S(1)}, u32[]{:S(2)}, u32[]{:S(2)}) %collective-permute-start.4) | collective-permute-done | bytes 217120 | tf_op jit(solution)/shard_map/ppermute | solution.py:26
  31.1 0.0 collective-permute-done.8.rest_4_
  31.1 2.7 %collective-permute-start.9 = (bf16[424,256]{1,0:T(8,128)(2,1)S(1)}, bf16[424,256]{1,0:T(8,128)(2,1)S(1)}, u32[]{:S(2)}, u32[]{:S(2)}) collective-permute-start(bf16[424,256]{1,0:T(8,128)(2,1)S(1)} %collective-permute-done.8.rest_4_), channel_id=1, source_target_pairs={{0,7},{1,0},{2,1},{3,2},{4,3},{5,4},{6,5},{7,6},{8,15},{9,8},{10,9... | collective-permute-start | bytes 651272 | tf_op jit(solution)/shard_map/ppermute | solution.py:26
  33.8 2.0 %collective-permute-done.12.rest_3_ = bf16[424,256]{1,0:T(8,128)(2,1)S(1)} collective-permute-done((bf16[424,256]{1,0:T(8,128)(2,1)S(1)}, bf16[424,256]{1,0:T(8,128)(2,1)S(1)}, u32[]{:S(2)}, u32[]{:S(2)}) %collective-permute-start.12) | collective-permute-done | bytes 217120 | tf_op jit(solution)/shard_map/ppermute | solution.py:26
  35.8 2.7 %collective-permute-start.17 = (bf16[424,256]{1,0:T(8,128)(2,1)S(1)}, bf16[424,256]{1,0:T(8,128)(2,1)S(1)}, u32[]{:S(2)}, u32[]{:S(2)}) collective-permute-start(bf16[424,256]{1,0:T(8,128)(2,1)S(1)} %collective-permute-done.16.rest_4_), channel_id=1, source_target_pairs={{0,7},{1,0},{2,1},{3,2},{4,3},{5,4},{6,5},{7,6},{8,15},{9,8},{10,9... | collective-permute-start | bytes 651272 | tf_op jit(solution)/shard_map/ppermute | solution.py:26
  38.4 1.9 %collective-permute-done.5.value_ref.rest_5_ = bf16[424,256]{1,0:T(8,128)(2,1)S(1)} collective-permute-done((bf16[424,256]{1,0:T(8,128)(2,1)S(1)}, bf16[424,256]{1,0:T(8,128)(2,1)S(1)}, u32[]{:S(2)}, u32[]{:S(2)}) %collective-permute-start.5) | collective-permute-done | bytes 217120 | tf_op jit(solution)/shard_map/ppermute | solution.py:26
  40.3 0.3 collective-permute-start.6
  40.6 2.7 %collective-permute-start.10 = (bf16[216,256]{1,0:T(8,128)(2,1)S(1)}, bf16[216,256]{1,0:T(8,128)(2,1)S(1)}, u32[]{:S(2)}, u32[]{:S(2)}) collective-permute-start(bf16[216,256]{1,0:T(8,128)(2,1)S(1)} %shard_map.70), channel_id=1, source_target_pairs={{0,7},{1,0},{2,1},{3,2},{4,3},{5,4},{6,5},{7,6},{8,15},{9,8},{10,9... | collective-permute-start | bytes 331784 | tf_op jit(solution)/shard_map/ppermute | solution.py:26
  43.3 0.8 convert_rsqrt_fusion
  44.1 0.2 broadcast_in_dim.5.scale_ref
  44.3 2.8 %convert.2.tile_0 = bf16[416,3392]{1,0:T(8,128)(2,1)S(1)} custom-call(s32[848,3392]{1,0:T(8,128)} %bitcast.6), custom_call_target="tpu_custom_call" | custom-call | flops 16777216 | bytes 9437184 | tf_op jit(solution)/shard_map/convert/pallas_call | solution.py:237
  47.1 2.9 %convert.3.tile_1 = bf16[432,3392]{1,0:T(8,128)(2,1)S(1)} custom-call(s32[848,3392]{1,0:T(8,128)} %bitcast.7), custom_call_target="tpu_custom_call" | custom-call | flops 16777216 | bytes 9437184 | tf_op jit(solution)/shard_map/convert/pallas_call | solution.py:237
  50.0 0.0 collective-permute-done.13.value_ref.rest_5_
  50.0 0.0 copy-start
  50.0 0.1 collective-permute-start.14
  50.1 0.0 collective-permute-done.17.value_ref.rest_6_
  50.1 2.7 %collective-permute-start.18 = (bf16[216,256]{1,0:T(8,128)(2,1)S(1)}, bf16[216,256]{1,0:T(8,128)(2,1)S(1)}, u32[]{:S(2)}, u32[]{:S(2)}) collective-permute-start(bf16[216,256]{1,0:T(8,128)(2,1)S(1)} %shard_map.74), channel_id=1, source_target_pairs={{0,7},{1,0},{2,1},{3,2},{4,3},{5,4},{6,5},{7,6},{8,15},{9,8},{10,9... | collective-permute-start | bytes 331784 | tf_op jit(solution)/shard_map/ppermute | solution.py:26
  52.9 0.2 shard_map.71
  53.1 0.2 shard_map.75
  53.3 0.0 collective-permute-done.6.rest_0_
  53.4 2.2 %shard_map.72 = (bf16[848,256]{1,0:T(8,128)(2,1)S(1)}, f32[256,512]{1,0:T(8,128)S(1)}, f32[3392,128]{1,0:T(8,128)S(1)}, f32[3392,128]{1,0:T(8,128)S(1)}) custom-call(s32[1]{0:T(128)} %bitcast.2.me_ref, bf16[416,3392]{1,0:T(8,128)(2,1)S(1)} %convert.2.tile_0, bf16[432,3392]{1,0:T(8,128)(2,1)S(1)} %convert.3.tile_1, ...), custom_call_target="tpu_custom_call", output_to_operand_aliasing={{2}: (7, {}), {3}: (8, {})} | custom-call | flops 1472724992 | bytes 1048576 | tf_op jit(solution)/shard_map/pallas_call | solution.py:30
  55.6 0.0 copy-start.1
  55.6 2.3 %shard_map.76 = (bf16[848,256]{1,0:T(8,128)(2,1)S(1)}, f32[4,64,512]{2,1,0:T(8,128)S(1)}, bf16[4,64,512]{2,1,0:T(8,128)(2,1)S(1)}, f32[3392,128]{1,0:T(8,128)S(1)}, f32[3392,128]{1,0:T(8,128)S(1)}) custom-call(s32[1]{0:T(128)} %bitcast.2.me_ref, s32[1]{0:T(128)} %bitcast.1.core_ref.me_ref, ...), custom_call_target="tpu_custom_call", output_to_operand_aliasing={{3}: (9, {}), {4}: (10, {})} | custom-call | flops 1472724992 | bytes 1048576 | tf_op jit(solution)/shard_map/pallas_call | solution.py:30
  57.9 5.5 %collective-permute-start.23 = (bf16[4,64,512]{2,1,0:T(8,128)(2,1)S(1)}, bf16[4,64,512]{2,1,0:T(8,128)(2,1)S(1)}, u32[]{:S(2)}, u32[]{:S(2)}) collective-permute-start(bf16[4,64,512]{2,1,0:T(8,128)(2,1)S(1)} %get-tuple-element.53), channel_id=1, source_target_pairs={{0,32},{32,0},{64,96},{96,64},{128,160},{160,128},{192,224},{224,1... | collective-permute-start | bytes 786440 | tf_op jit(solution)/shard_map/ppermute | solution.py:197
  63.4 0.8 shard_map.77
  64.3 0.1 collective-permute-start.19
  64.4 0.2 collective-permute-done.23.got_ref
  64.6 0.1 shard_map.80
  64.7 1.4 %collective-permute-start.24 = (bf16[64,512]{1,0:T(8,128)(2,1)S(1)}, bf16[64,512]{1,0:T(8,128)(2,1)S(1)}, u32[]{:S(2)}, u32[]{:S(2)}) collective-permute-start(bf16[64,512]{1,0:T(8,128)(2,1)S(1)} %get-tuple-element.55), channel_id=1, source_target_pairs={{0,64},{32,96},{64,128},{96,160},{128,192},{160,224},{192,0},{224,... | collective-permute-start | bytes 196616 | tf_op jit(solution)/shard_map/ppermute | solution.py:203
  66.0 2.6 %collective-permute-start.25 = (bf16[64,512]{1,0:T(8,128)(2,1)S(1)}, bf16[64,512]{1,0:T(8,128)(2,1)S(1)}, u32[]{:S(2)}, u32[]{:S(2)}) collective-permute-start(bf16[64,512]{1,0:T(8,128)(2,1)S(1)} %get-tuple-element.56), channel_id=1, source_target_pairs={{0,128},{32,160},{64,192},{96,224},{128,0},{160,32},{192,64},{224,... | collective-permute-start | bytes 196616 | tf_op jit(solution)/shard_map/ppermute | solution.py:203
  68.7 1.1 %collective-permute-start.26 = (bf16[64,512]{1,0:T(8,128)(2,1)S(1)}, bf16[64,512]{1,0:T(8,128)(2,1)S(1)}, u32[]{:S(2)}, u32[]{:S(2)}) collective-permute-start(bf16[64,512]{1,0:T(8,128)(2,1)S(1)} %get-tuple-element.57), channel_id=1, source_target_pairs={{0,192},{32,224},{64,0},{96,32},{128,64},{160,96},{192,128},{224,1... | collective-permute-start | bytes 196616 | tf_op jit(solution)/shard_map/ppermute | solution.py:203
  69.7 1.8 %collective-permute-done.25.rest_1_ = bf16[64,512]{1,0:T(8,128)(2,1)S(1)} collective-permute-done((bf16[64,512]{1,0:T(8,128)(2,1)S(1)}, bf16[64,512]{1,0:T(8,128)(2,1)S(1)}, u32[]{:S(2)}, u32[]{:S(2)}) %collective-permute-start.25) | collective-permute-done | bytes 65568 | tf_op jit(solution)/shard_map/ppermute | solution.py:203
  71.6 0.5 collective-permute-done.26.rest_2_
  72.1 0.9 shard_map.81
  72.9 8.4 %all-to-all-start = ((f32[32,8,128]{2,1,0:T(8,128)}), f32[32,8,128]{2,1,0:T(8,128)S(1)}, u32[]{:S(2)}, u32[]{:S(2)}) async-start(f32[32,8,128]{2,1,0:T(8,128)} %shard_map.81), calls=%async_computation | async-start | bytes 262144 | tf_op jit(solution)/shard_map/all_to_all | solution.py:340
  81.4 0.1 shard_map.78
  81.4 0.1 collective-permute-start.20
  81.5 3.2 %collective-permute-start.21 = (bf16[64,848]{1,0:T(8,128)(2,1)S(1)}, bf16[64,848]{1,0:T(8,128)(2,1)S(1)}, u32[]{:S(2)}, u32[]{:S(2)}) collective-permute-start(bf16[64,848]{1,0:T(8,128)(2,1)S(1)} %get-tuple-element.50), channel_id=1, source_target_pairs={{0,128},{32,160},{64,192},{96,224},{128,0},{160,32},{192,64},{224,... | collective-permute-start | bytes 325640 | tf_op jit(solution)/shard_map/ppermute | solution.py:203
  84.7 0.4 collective-permute-start.22
  85.1 1.3 %collective-permute-done.20.rest_0_ = bf16[64,848]{1,0:T(8,128)(2,1)S(1)} collective-permute-done((bf16[64,848]{1,0:T(8,128)(2,1)S(1)}, bf16[64,848]{1,0:T(8,128)(2,1)S(1)}, u32[]{:S(2)}, u32[]{:S(2)}) %collective-permute-start.20) | collective-permute-done | bytes 108576 | tf_op jit(solution)/shard_map/ppermute | solution.py:203
  86.4 1.9 %collective-permute-done.21.rest_1_ = bf16[64,848]{1,0:T(8,128)(2,1)S(1)} collective-permute-done((bf16[64,848]{1,0:T(8,128)(2,1)S(1)}, bf16[64,848]{1,0:T(8,128)(2,1)S(1)}, u32[]{:S(2)}, u32[]{:S(2)}) %collective-permute-start.21) | collective-permute-done | bytes 108576 | tf_op jit(solution)/shard_map/ppermute | solution.py:203
  88.3 0.4 collective-permute-done.22.rest_2_
  88.6 0.7 shard_map.79
  89.3 1.1 %all-to-all-done.pieces_ref = f32[32,8,128]{2,1,0:T(8,128)S(1)} async-done(((f32[32,8,128]{2,1,0:T(8,128)}), f32[32,8,128]{2,1,0:T(8,128)S(1)}, u32[]{:S(2)}, u32[]{:S(2)}) %all-to-all-start) | async-done | bytes 131104 | tf_op jit(solution)/shard_map/all_to_all | solution.py:340
  90.5 0.7 shard_map.82
  (17 shorter events, 0.1 us)
Async XLA Ops:
  2.4 5.7 %collective-permute-start = (bf16[106,512]{1,0:T(8,128)(2,1)S(1)}, bf16[106,512]{1,0:T(8,128)(2,1)S(1)}, u32[]{:S(2)}, u32[]{:S(2)}) collective-permute-start(bf16[106,512]{1,0:T(8,128)(2,1)S(1)} %multiply_convert_fusion.refs_0_), channel_id=1, source_target_pairs={{0,8},{8,16},{16,24},{24,0},{1,9},{9,17},{17,25},{25,1},{2,10},{10... | collective-permute-start | bytes 325640 | tf_op jit(solution)/shard_map/ppermute | solution.py:26
  4.5 7.5 %collective-permute-start.1 = (bf16[106,512]{1,0:T(8,128)(2,1)S(1)}, bf16[106,512]{1,0:T(8,128)(2,1)S(1)}, u32[]{:S(2)}, u32[]{:S(2)}) collective-permute-start(bf16[106,512]{1,0:T(8,128)(2,1)S(1)} %multiply_convert_fusion.refs_0_), channel_id=1, source_target_pairs={{0,16},{8,24},{16,0},{24,8},{1,17},{9,25},{17,1},{25,9},{2,18},{10... | collective-permute-start | bytes 325640 | tf_op jit(solution)/shard_map/ppermute | solution.py:26
  7.0 5.0 %collective-permute-start.2 = (bf16[106,512]{1,0:T(8,128)(2,1)S(1)}, bf16[106,512]{1,0:T(8,128)(2,1)S(1)}, u32[]{:S(2)}, u32[]{:S(2)}) collective-permute-start(bf16[106,512]{1,0:T(8,128)(2,1)S(1)} %multiply_convert_fusion.refs_0_), channel_id=1, source_target_pairs={{0,24},{8,0},{16,8},{24,16},{1,25},{9,1},{17,9},{25,17},{2,26},{10... | collective-permute-start | bytes 325640 | tf_op jit(solution)/shard_map/ppermute | solution.py:26
  12.1 9.8 %collective-permute-start.3 = (bf16[424,256]{1,0:T(8,128)(2,1)S(1)}, bf16[424,256]{1,0:T(8,128)(2,1)S(1)}, u32[]{:S(2)}, u32[]{:S(2)}) collective-permute-start(bf16[424,256]{1,0:T(8,128)(2,1)S(1)} %get-tuple-element.37.rest_0_), channel_id=1, source_target_pairs={{0,1},{1,2},{2,3},{3,4},{4,5},{5,6},{6,7},{7,0},{8,9},{9,10},{10,1... | collective-permute-start | bytes 651272 | tf_op jit(solution)/shard_map/ppermute | solution.py:26
  13.8 8.1 %collective-permute-start.7 = (bf16[424,256]{1,0:T(8,128)(2,1)S(1)}, bf16[424,256]{1,0:T(8,128)(2,1)S(1)}, u32[]{:S(2)}, u32[]{:S(2)}) collective-permute-start(bf16[424,256]{1,0:T(8,128)(2,1)S(1)} %get-tuple-element.37.rest_0_), channel_id=1, source_target_pairs={{0,7},{1,0},{2,1},{3,2},{4,3},{5,4},{6,5},{7,6},{8,15},{9,8},{10,9... | collective-permute-start | bytes 651272 | tf_op jit(solution)/shard_map/ppermute | solution.py:26
  17.8 8.8 %collective-permute-start.11 = (bf16[424,256]{1,0:T(8,128)(2,1)S(1)}, bf16[424,256]{1,0:T(8,128)(2,1)S(1)}, u32[]{:S(2)}, u32[]{:S(2)}) collective-permute-start(bf16[424,256]{1,0:T(8,128)(2,1)S(1)} %get-tuple-element.42.rest_0_), channel_id=1, source_target_pairs={{0,1},{1,2},{2,3},{3,4},{4,5},{5,6},{6,7},{7,0},{8,9},{9,10},{10,1... | collective-permute-start | bytes 651272 | tf_op jit(solution)/shard_map/ppermute | solution.py:26
  17.8 8.8 %collective-permute-start.15 = (bf16[424,256]{1,0:T(8,128)(2,1)S(1)}, bf16[424,256]{1,0:T(8,128)(2,1)S(1)}, u32[]{:S(2)}, u32[]{:S(2)}) collective-permute-start(bf16[424,256]{1,0:T(8,128)(2,1)S(1)} %get-tuple-element.42.rest_0_), channel_id=1, source_target_pairs={{0,7},{1,0},{2,1},{3,2},{4,3},{5,4},{6,5},{7,6},{8,15},{9,8},{10,9... | collective-permute-start | bytes 651272 | tf_op jit(solution)/shard_map/ppermute | solution.py:26
  21.9 9.2 %collective-permute-start.4 = (bf16[424,256]{1,0:T(8,128)(2,1)S(1)}, bf16[424,256]{1,0:T(8,128)(2,1)S(1)}, u32[]{:S(2)}, u32[]{:S(2)}) collective-permute-start(bf16[424,256]{1,0:T(8,128)(2,1)S(1)} %collective-permute-done.3.rest_1_), channel_id=1, source_target_pairs={{0,1},{1,2},{2,3},{3,4},{4,5},{5,6},{6,7},{7,0},{8,9},{9,10},{10,1... | collective-permute-start | bytes 651272 | tf_op jit(solution)/shard_map/ppermute | solution.py:26
  21.9 9.2 %collective-permute-start.8 = (bf16[424,256]{1,0:T(8,128)(2,1)S(1)}, bf16[424,256]{1,0:T(8,128)(2,1)S(1)}, u32[]{:S(2)}, u32[]{:S(2)}) collective-permute-start(bf16[424,256]{1,0:T(8,128)(2,1)S(1)} %collective-permute-done.7.rest_2_), channel_id=1, source_target_pairs={{0,7},{1,0},{2,1},{3,2},{4,3},{5,4},{6,5},{7,6},{8,15},{9,8},{10,9... | collective-permute-start | bytes 651272 | tf_op jit(solution)/shard_map/ppermute | solution.py:26
  26.6 9.2 %collective-permute-start.12 = (bf16[424,256]{1,0:T(8,128)(2,1)S(1)}, bf16[424,256]{1,0:T(8,128)(2,1)S(1)}, u32[]{:S(2)}, u32[]{:S(2)}) collective-permute-start(bf16[424,256]{1,0:T(8,128)(2,1)S(1)} %collective-permute-done.11.rest_1_), channel_id=1, source_target_pairs={{0,1},{1,2},{2,3},{3,4},{4,5},{5,6},{6,7},{7,0},{8,9},{9,10},{10,1... | collective-permute-start | bytes 651272 | tf_op jit(solution)/shard_map/ppermute | solution.py:26
  26.6 9.2 %collective-permute-start.16 = (bf16[424,256]{1,0:T(8,128)(2,1)S(1)}, bf16[424,256]{1,0:T(8,128)(2,1)S(1)}, u32[]{:S(2)}, u32[]{:S(2)}) collective-permute-start(bf16[424,256]{1,0:T(8,128)(2,1)S(1)} %collective-permute-done.15.rest_2_), channel_id=1, source_target_pairs={{0,7},{1,0},{2,1},{3,2},{4,3},{5,4},{6,5},{7,6},{8,15},{9,8},{10,9... | collective-permute-start | bytes 651272 | tf_op jit(solution)/shard_map/ppermute | solution.py:26
  31.1 9.2 %collective-permute-start.5 = (bf16[424,256]{1,0:T(8,128)(2,1)S(1)}, bf16[424,256]{1,0:T(8,128)(2,1)S(1)}, u32[]{:S(2)}, u32[]{:S(2)}) collective-permute-start(bf16[424,256]{1,0:T(8,128)(2,1)S(1)} %collective-permute-done.4.rest_3_), channel_id=1, source_target_pairs={{0,1},{1,2},{2,3},{3,4},{4,5},{5,6},{6,7},{7,0},{8,9},{9,10},{10,1... | collective-permute-start | bytes 651272 | tf_op jit(solution)/shard_map/ppermute | solution.py:26
  31.1 9.5 %collective-permute-start.9 = (bf16[424,256]{1,0:T(8,128)(2,1)S(1)}, bf16[424,256]{1,0:T(8,128)(2,1)S(1)}, u32[]{:S(2)}, u32[]{:S(2)}) collective-permute-start(bf16[424,256]{1,0:T(8,128)(2,1)S(1)} %collective-permute-done.8.rest_4_), channel_id=1, source_target_pairs={{0,7},{1,0},{2,1},{3,2},{4,3},{5,4},{6,5},{7,6},{8,15},{9,8},{10,9... | collective-permute-start | bytes 651272 | tf_op jit(solution)/shard_map/ppermute | solution.py:26
  35.8 14.2 %collective-permute-start.13 = (bf16[424,256]{1,0:T(8,128)(2,1)S(1)}, bf16[424,256]{1,0:T(8,128)(2,1)S(1)}, u32[]{:S(2)}, u32[]{:S(2)}) collective-permute-start(bf16[424,256]{1,0:T(8,128)(2,1)S(1)} %collective-permute-done.12.rest_3_), channel_id=1, source_target_pairs={{0,1},{1,2},{2,3},{3,4},{4,5},{5,6},{6,7},{7,0},{8,9},{9,10},{10,1... | collective-permute-start | bytes 651272 | tf_op jit(solution)/shard_map/ppermute | solution.py:26
  35.8 14.4 %collective-permute-start.17 = (bf16[424,256]{1,0:T(8,128)(2,1)S(1)}, bf16[424,256]{1,0:T(8,128)(2,1)S(1)}, u32[]{:S(2)}, u32[]{:S(2)}) collective-permute-start(bf16[424,256]{1,0:T(8,128)(2,1)S(1)} %collective-permute-done.16.rest_4_), channel_id=1, source_target_pairs={{0,7},{1,0},{2,1},{3,2},{4,3},{5,4},{6,5},{7,6},{8,15},{9,8},{10,9... | collective-permute-start | bytes 651272 | tf_op jit(solution)/shard_map/ppermute | solution.py:26
  40.3 13.0 %collective-permute-start.6 = (bf16[208,256]{1,0:T(8,128)(2,1)S(1)}, bf16[208,256]{1,0:T(8,128)(2,1)S(1)}, u32[]{:S(2)}, u32[]{:S(2)}) collective-permute-start(bf16[208,256]{1,0:T(8,128)(2,1)S(1)} %shard_map.69), channel_id=1, source_target_pairs={{0,1},{1,2},{2,3},{3,4},{4,5},{5,6},{6,7},{7,0},{8,9},{9,10},{10,1... | collective-permute-start | bytes 319496 | tf_op jit(solution)/shard_map/ppermute | solution.py:26
  40.6 12.7 %collective-permute-start.10 = (bf16[216,256]{1,0:T(8,128)(2,1)S(1)}, bf16[216,256]{1,0:T(8,128)(2,1)S(1)}, u32[]{:S(2)}, u32[]{:S(2)}) collective-permute-start(bf16[216,256]{1,0:T(8,128)(2,1)S(1)} %shard_map.70), channel_id=1, source_target_pairs={{0,7},{1,0},{2,1},{3,2},{4,3},{5,4},{6,5},{7,6},{8,15},{9,8},{10,9... | collective-permute-start | bytes 331784 | tf_op jit(solution)/shard_map/ppermute | solution.py:26
  50.0 3.3 %copy-start = (bf16[848,512]{1,0:T(8,128)(2,1)S(1)}, bf16[848,512]{1,0:T(8,128)(2,1)}, u32[]{:S(2)}) copy-start(bf16[848,512]{1,0:T(8,128)(2,1)} %features_ref.3) | copy-start | bytes 2605060
  50.0 5.6 %collective-permute-start.14 = (bf16[208,256]{1,0:T(8,128)(2,1)S(1)}, bf16[208,256]{1,0:T(8,128)(2,1)S(1)}, u32[]{:S(2)}, u32[]{:S(2)}) collective-permute-start(bf16[208,256]{1,0:T(8,128)(2,1)S(1)} %shard_map.73), channel_id=1, source_target_pairs={{0,1},{1,2},{2,3},{3,4},{4,5},{5,6},{6,7},{7,0},{8,9},{9,10},{10,1... | collective-permute-start | bytes 319496 | tf_op jit(solution)/shard_map/ppermute | solution.py:26
  50.1 5.5 %collective-permute-start.18 = (bf16[216,256]{1,0:T(8,128)(2,1)S(1)}, bf16[216,256]{1,0:T(8,128)(2,1)S(1)}, u32[]{:S(2)}, u32[]{:S(2)}) collective-permute-start(bf16[216,256]{1,0:T(8,128)(2,1)S(1)} %shard_map.74), channel_id=1, source_target_pairs={{0,7},{1,0},{2,1},{3,2},{4,3},{5,4},{6,5},{7,6},{8,15},{9,8},{10,9... | collective-permute-start | bytes 331784 | tf_op jit(solution)/shard_map/ppermute | solution.py:26
  55.6 7.8 %copy-start.1 = (bf16[512,512]{1,0:T(8,128)(2,1)S(1)}, bf16[512,512]{1,0:T(8,128)(2,1)}, u32[]{:S(2)}) copy-start(bf16[512,512]{1,0:T(8,128)(2,1)} %weight_ref.1) | copy-start | bytes 1572868
  57.9 6.7 %collective-permute-start.23 = (bf16[4,64,512]{2,1,0:T(8,128)(2,1)S(1)}, bf16[4,64,512]{2,1,0:T(8,128)(2,1)S(1)}, u32[]{:S(2)}, u32[]{:S(2)}) collective-permute-start(bf16[4,64,512]{2,1,0:T(8,128)(2,1)S(1)} %get-tuple-element.53), channel_id=1, source_target_pairs={{0,32},{32,0},{64,96},{96,64},{128,160},{160,128},{192,224},{224,1... | collective-permute-start | bytes 786440 | tf_op jit(solution)/shard_map/ppermute | solution.py:197
  64.3 17.0 %collective-permute-start.19 = (bf16[4,64,848]{2,1,0:T(8,128)(2,1)S(1)}, bf16[4,64,848]{2,1,0:T(8,128)(2,1)S(1)}, u32[]{:S(2)}, u32[]{:S(2)}) collective-permute-start(bf16[4,64,848]{2,1,0:T(8,128)(2,1)S(1)} %get-tuple-element.47), channel_id=1, source_target_pairs={{0,32},{32,0},{64,96},{96,64},{128,160},{160,128},{192,224},{224,1... | collective-permute-start | bytes 1302536 | tf_op jit(solution)/shard_map/ppermute | solution.py:197
  64.7 5.1 %collective-permute-start.24 = (bf16[64,512]{1,0:T(8,128)(2,1)S(1)}, bf16[64,512]{1,0:T(8,128)(2,1)S(1)}, u32[]{:S(2)}, u32[]{:S(2)}) collective-permute-start(bf16[64,512]{1,0:T(8,128)(2,1)S(1)} %get-tuple-element.55), channel_id=1, source_target_pairs={{0,64},{32,96},{64,128},{96,160},{128,192},{160,224},{192,0},{224,... | collective-permute-start | bytes 196616 | tf_op jit(solution)/shard_map/ppermute | solution.py:203
  66.0 5.5 %collective-permute-start.25 = (bf16[64,512]{1,0:T(8,128)(2,1)S(1)}, bf16[64,512]{1,0:T(8,128)(2,1)S(1)}, u32[]{:S(2)}, u32[]{:S(2)}) collective-permute-start(bf16[64,512]{1,0:T(8,128)(2,1)S(1)} %get-tuple-element.56), channel_id=1, source_target_pairs={{0,128},{32,160},{64,192},{96,224},{128,0},{160,32},{192,64},{224,... | collective-permute-start | bytes 196616 | tf_op jit(solution)/shard_map/ppermute | solution.py:203
  68.7 3.4 %collective-permute-start.26 = (bf16[64,512]{1,0:T(8,128)(2,1)S(1)}, bf16[64,512]{1,0:T(8,128)(2,1)S(1)}, u32[]{:S(2)}, u32[]{:S(2)}) collective-permute-start(bf16[64,512]{1,0:T(8,128)(2,1)S(1)} %get-tuple-element.57), channel_id=1, source_target_pairs={{0,192},{32,224},{64,0},{96,32},{128,64},{160,96},{192,128},{224,1... | collective-permute-start | bytes 196616 | tf_op jit(solution)/shard_map/ppermute | solution.py:203
  72.9 17.6 %all-to-all-start = ((f32[32,8,128]{2,1,0:T(8,128)}), f32[32,8,128]{2,1,0:T(8,128)S(1)}, u32[]{:S(2)}, u32[]{:S(2)}) async-start(f32[32,8,128]{2,1,0:T(8,128)} %shard_map.81), calls=%async_computation | async-start | bytes 262144 | tf_op jit(solution)/shard_map/all_to_all | solution.py:340
  81.4 4.9 %collective-permute-start.20 = (bf16[64,848]{1,0:T(8,128)(2,1)S(1)}, bf16[64,848]{1,0:T(8,128)(2,1)S(1)}, u32[]{:S(2)}, u32[]{:S(2)}) collective-permute-start(bf16[64,848]{1,0:T(8,128)(2,1)S(1)} %get-tuple-element.49), channel_id=1, source_target_pairs={{0,64},{32,96},{64,128},{96,160},{128,192},{160,224},{192,0},{224,... | collective-permute-start | bytes 325640 | tf_op jit(solution)/shard_map/ppermute | solution.py:203
  81.5 6.7 %collective-permute-start.21 = (bf16[64,848]{1,0:T(8,128)(2,1)S(1)}, bf16[64,848]{1,0:T(8,128)(2,1)S(1)}, u32[]{:S(2)}, u32[]{:S(2)}) collective-permute-start(bf16[64,848]{1,0:T(8,128)(2,1)S(1)} %get-tuple-element.50), channel_id=1, source_target_pairs={{0,128},{32,160},{64,192},{96,224},{128,0},{160,32},{192,64},{224,... | collective-permute-start | bytes 325640 | tf_op jit(solution)/shard_map/ppermute | solution.py:203
  84.7 3.9 %collective-permute-start.22 = (bf16[64,848]{1,0:T(8,128)(2,1)S(1)}, bf16[64,848]{1,0:T(8,128)(2,1)S(1)}, u32[]{:S(2)}, u32[]{:S(2)}) collective-permute-start(bf16[64,848]{1,0:T(8,128)(2,1)S(1)} %get-tuple-element.51), channel_id=1, source_target_pairs={{0,192},{32,224},{64,0},{96,32},{128,64},{160,96},{192,128},{224,1... | collective-permute-start | bytes 325640 | tf_op jit(solution)/shard_map/ppermute | solution.py:203

commit v3 on v2

--- a/solution.py
+++ b/solution.py
@@ -179,16 +179,13 @@
     out_ref[:, :, share:] = blocks[:, lines:]
 
 
-def unpack_kernel(pieces_ref, out_ref):
-    lines, share = pieces_ref.shape[1], out_ref.shape[1]
+def last_kernel(pieces_ref, own_ref, *rest):
+    *refs, weight_ref, input_ref = rest
+    input_ref[...] = added(own_ref, refs).astype(input_ref.dtype)
+    lines, share = pieces_ref.shape[1], weight_ref.shape[1]
     total = pieces_ref[...].sum(axis=0)
-    out_ref[:lines, :] = total[:, :share]
-    out_ref[lines:, :] = total[:, share:]
-
-
-def sum_kernel(own_ref, *rest):
-    *refs, out_ref = rest
-    out_ref[...] = added(own_ref, refs).astype(out_ref.dtype)
+    weight_ref[:lines, :] = total[:, :share]
+    weight_ref[lines:, :] = total[:, share:]
 
 
 def over_rows(me, keep, send, n_y):
@@ -318,10 +315,7 @@
     )
     q_keep, q_send = call(
         q_kernel,
-        (
-            jax.ShapeDtypeStruct((n_y, share, cols_here), jnp.float32),
-            unit((n_y, share, cols_here)),
-        ),
+        (jax.ShapeDtypeStruct((n_y, share, cols_here), jnp.float32), unit((n_y, share, cols_here))),
         (core.reshape(1), first, second, weight),
         scratch=(pltpu.VMEM((n_row, share, cols_here), jnp.float32),),
         flops=2 * cols_here * width * width,
@@ -338,11 +332,13 @@
         smem=0,
     )
     w_pieces = lax.all_to_all(packed, COL, split_axis=0, concat_axis=0, tiled=True)
-    grad_weight = call(
-        unpack_kernel, jax.ShapeDtypeStruct((2 * lines, share), jnp.float32), (w_pieces,), smem=0
-    )
-    grad_input = call(sum_kernel, unit((share, cols_here)), (q_own, *q_parts), smem=0).T
-    return (grad_input, grad_weight)
+    grad_weight, grad_input = call(
+        last_kernel,
+        (jax.ShapeDtypeStruct((2 * lines, share), jnp.float32), unit((share, cols_here))),
+        (w_pieces, q_own, *q_parts),
+        smem=0,
+    )
+    return (grad_input.T, grad_weight)
 
 
 def solution(mesh):

time: 93 us -> 92.9 us (level)
    pallas_call x15 -> x14, Pallas kernels: 8.33 us -> 7.69 us  [call(): pl.pallas_call(body, out_shape=out, in_specs=[SMEM] * smem + [VMEM] * (le...]
  transfers between devices with their start and end apart: 28 -> 28, of which waited for: 13 -> 13; matrix products, arithmetic and copies ran while one was open for 1% -> 1% of each run, Pallas kernels for 12% -> 11%
where the time goes in v3:
time: 92.9 us; the launch traced here: 91.3 us
  starting transfers between devices  53.4 us (57%)
  waiting for transfers between devices  20.9 us (22%)
  Pallas kernels  13.4 us (14%)
  other arithmetic  2.53 us (3%)
    ppermute x19, starting transfers between devices, shifted(): return lax.ppermute(value, axis, [(i, (i + step) % n) for i in range(n)])  30.6 us
    ppermute x19, waiting for transfers between devices, shifted(): return lax.ppermute(value, axis, [(i, (i + step) % n) for i in range(n)])  13 us
    ppermute x6, starting transfers between devices, over_rows(): lax.ppermute(part, 'row', [(i, (i + CORES * step) % n) for i in range(n)])  8.7 us
    all_to_all x1, starting transfers between devices, per_device(): lax.all_to_all(packed, COL, split_axis=0, concat_axis=0, tiled=True)  8.4 us
    pallas_call x14, Pallas kernels, call(): pl.pallas_call(body, out_shape=out, in_specs=[SMEM] * smem + [VMEM] * (le...  7.69 us
    ppermute x6, waiting for transfers between devices, over_rows(): lax.ppermute(part, 'row', [(i, (i + CORES * step) % n) for i in range(n)])  5.89 us
    pallas_call x2, Pallas kernels, converted(): pl.pallas_call(functools.partial(convert_kernel, start), out_shape=jax.Sh...  5.7 us
    ppermute x2, starting transfers between devices, over_rows(): got = lax.ppermute(send, 'row', [(i, i ^ 1) for i in range(n)])  5.61 us
  transfers between devices with their start and end apart: 28, of which 13 were waited for; matrix products, arithmetic and copies ran while one was open for 1% of the time, Pallas kernels for 11%

profile of v3, /device:TPU:1, one launch (start us, length us, event | category | flops | bytes accessed | tf_op | source)
XLA Modules:
  0.0 91.3 jit_solution(10062947973689806725)
XLA Ops:
  0.6 0.8 convert_rsqrt_fusion.1
  1.4 1.0 %multiply_convert_fusion.refs_0_ = bf16[106,512]{1,0:T(8,128)(2,1)S(1)} fusion(bf16[106,512]{1,0:T(8,128)(2,1)} %param.7, f32[106]{0:T(128)S(1)} %convert_rsqrt_fusion.1), kind=kLoop, calls=%fused_computation | loop fusion | flops 162816 | bytes 217512 | tf_op jit(solution)/shard_map/convert_element_type | solution.py:230
  2.4 2.1 %collective-permute-start = (bf16[106,512]{1,0:T(8,128)(2,1)S(1)}, bf16[106,512]{1,0:T(8,128)(2,1)S(1)}, u32[]{:S(2)}, u32[]{:S(2)}) collective-permute-start(bf16[106,512]{1,0:T(8,128)(2,1)S(1)} %multiply_convert_fusion.refs_0_), channel_id=1, source_target_pairs={{0,8},{8,16},{16,24},{24,0},{1,9},{9,17},{17,25},{25,1},{2,10},{10... | collective-permute-start | bytes 325640 | tf_op jit(solution)/shard_map/ppermute | solution.py:26
  4.5 2.5 %collective-permute-start.1 = (bf16[106,512]{1,0:T(8,128)(2,1)S(1)}, bf16[106,512]{1,0:T(8,128)(2,1)S(1)}, u32[]{:S(2)}, u32[]{:S(2)}) collective-permute-start(bf16[106,512]{1,0:T(8,128)(2,1)S(1)} %multiply_convert_fusion.refs_0_), channel_id=1, source_target_pairs={{0,16},{8,24},{16,0},{24,8},{1,17},{9,25},{17,1},{25,9},{2,18},{10... | collective-permute-start | bytes 325640 | tf_op jit(solution)/shard_map/ppermute | solution.py:26
  7.0 1.2 %collective-permute-start.2 = (bf16[106,512]{1,0:T(8,128)(2,1)S(1)}, bf16[106,512]{1,0:T(8,128)(2,1)S(1)}, u32[]{:S(2)}, u32[]{:S(2)}) collective-permute-start(bf16[106,512]{1,0:T(8,128)(2,1)S(1)} %multiply_convert_fusion.refs_0_), channel_id=1, source_target_pairs={{0,24},{8,0},{16,8},{24,16},{1,25},{9,1},{17,9},{25,17},{2,26},{10... | collective-permute-start | bytes 325640 | tf_op jit(solution)/shard_map/ppermute | solution.py:26
  8.1 0.0 collective-permute-done.refs_1_
  8.1 3.9 %collective-permute-done.1.refs_2_ = bf16[106,512]{1,0:T(8,128)(2,1)S(1)} collective-permute-done((bf16[106,512]{1,0:T(8,128)(2,1)S(1)}, bf16[106,512]{1,0:T(8,128)(2,1)S(1)}, u32[]{:S(2)}, u32[]{:S(2)}) %collective-permute-start.1) | collective-permute-done | bytes 108576 | tf_op jit(solution)/shard_map/ppermute | solution.py:26
  12.0 0.1 shard_map.68
  12.1 1.7 %collective-permute-start.3 = (bf16[424,256]{1,0:T(8,128)(2,1)S(1)}, bf16[424,256]{1,0:T(8,128)(2,1)S(1)}, u32[]{:S(2)}, u32[]{:S(2)}) collective-permute-start(bf16[424,256]{1,0:T(8,128)(2,1)S(1)} %get-tuple-element.39.rest_0_), channel_id=1, source_target_pairs={{0,1},{1,2},{2,3},{3,4},{4,5},{5,6},{6,7},{7,0},{8,9},{9,10},{10,1... | collective-permute-start | bytes 651272 | tf_op jit(solution)/shard_map/ppermute | solution.py:26
  13.8 4.0 %collective-permute-start.7 = (bf16[424,256]{1,0:T(8,128)(2,1)S(1)}, bf16[424,256]{1,0:T(8,128)(2,1)S(1)}, u32[]{:S(2)}, u32[]{:S(2)}) collective-permute-start(bf16[424,256]{1,0:T(8,128)(2,1)S(1)} %get-tuple-element.39.rest_0_), channel_id=1, source_target_pairs={{0,7},{1,0},{2,1},{3,2},{4,3},{5,4},{6,5},{7,6},{8,15},{9,8},{10,9... | collective-permute-start | bytes 651272 | tf_op jit(solution)/shard_map/ppermute | solution.py:26
  17.8 0.0 collective-permute-start.11
  17.8 2.7 %collective-permute-start.15 = (bf16[424,256]{1,0:T(8,128)(2,1)S(1)}, bf16[424,256]{1,0:T(8,128)(2,1)S(1)}, u32[]{:S(2)}, u32[]{:S(2)}) collective-permute-start(bf16[424,256]{1,0:T(8,128)(2,1)S(1)} %get-tuple-element.43.rest_0_), channel_id=1, source_target_pairs={{0,7},{1,0},{2,1},{3,2},{4,3},{5,4},{6,5},{7,6},{8,15},{9,8},{10,9... | collective-permute-start | bytes 651272 | tf_op jit(solution)/shard_map/ppermute | solution.py:26
  20.5 1.4 %collective-permute-done.3.rest_1_ = bf16[424,256]{1,0:T(8,128)(2,1)S(1)} collective-permute-done((bf16[424,256]{1,0:T(8,128)(2,1)S(1)}, bf16[424,256]{1,0:T(8,128)(2,1)S(1)}, u32[]{:S(2)}, u32[]{:S(2)}) %collective-permute-start.3) | collective-permute-done | bytes 217120 | tf_op jit(solution)/shard_map/ppermute | solution.py:26
  21.9 0.0 collective-permute-start.4
  21.9 0.0 collective-permute-done.7.rest_2_
  21.9 2.7 %collective-permute-start.8 = (bf16[424,256]{1,0:T(8,128)(2,1)S(1)}, bf16[424,256]{1,0:T(8,128)(2,1)S(1)}, u32[]{:S(2)}, u32[]{:S(2)}) collective-permute-start(bf16[424,256]{1,0:T(8,128)(2,1)S(1)} %collective-permute-done.7.rest_2_), channel_id=1, source_target_pairs={{0,7},{1,0},{2,1},{3,2},{4,3},{5,4},{6,5},{7,6},{8,15},{9,8},{10,9... | collective-permute-start | bytes 651272 | tf_op jit(solution)/shard_map/ppermute | solution.py:26
  24.6 2.0 %collective-permute-done.11.rest_1_ = bf16[424,256]{1,0:T(8,128)(2,1)S(1)} collective-permute-done((bf16[424,256]{1,0:T(8,128)(2,1)S(1)}, bf16[424,256]{1,0:T(8,128)(2,1)S(1)}, u32[]{:S(2)}, u32[]{:S(2)}) %collective-permute-start.11) | collective-permute-done | bytes 217120 | tf_op jit(solution)/shard_map/ppermute | solution.py:26
  26.6 0.0 collective-permute-start.12
  26.6 2.7 %collective-permute-start.16 = (bf16[424,256]{1,0:T(8,128)(2,1)S(1)}, bf16[424,256]{1,0:T(8,128)(2,1)S(1)}, u32[]{:S(2)}, u32[]{:S(2)}) collective-permute-start(bf16[424,256]{1,0:T(8,128)(2,1)S(1)} %collective-permute-done.15.rest_2_), channel_id=1, source_target_pairs={{0,7},{1,0},{2,1},{3,2},{4,3},{5,4},{6,5},{7,6},{8,15},{9,8},{10,9... | collective-permute-start | bytes 651272 | tf_op jit(solution)/shard_map/ppermute | solution.py:26
  29.3 1.8 %collective-permute-done.4.rest_3_ = bf16[424,256]{1,0:T(8,128)(2,1)S(1)} collective-permute-done((bf16[424,256]{1,0:T(8,128)(2,1)S(1)}, bf16[424,256]{1,0:T(8,128)(2,1)S(1)}, u32[]{:S(2)}, u32[]{:S(2)}) %collective-permute-start.4) | collective-permute-done | bytes 217120 | tf_op jit(solution)/shard_map/ppermute | solution.py:26
  31.1 0.0 collective-permute-done.8.rest_4_
  31.1 2.7 %collective-permute-start.9 = (bf16[424,256]{1,0:T(8,128)(2,1)S(1)}, bf16[424,256]{1,0:T(8,128)(2,1)S(1)}, u32[]{:S(2)}, u32[]{:S(2)}) collective-permute-start(bf16[424,256]{1,0:T(8,128)(2,1)S(1)} %collective-permute-done.8.rest_4_), channel_id=1, source_target_pairs={{0,7},{1,0},{2,1},{3,2},{4,3},{5,4},{6,5},{7,6},{8,15},{9,8},{10,9... | collective-permute-start | bytes 651272 | tf_op jit(solution)/shard_map/ppermute | solution.py:26
  33.8 2.0 %collective-permute-done.12.rest_3_ = bf16[424,256]{1,0:T(8,128)(2,1)S(1)} collective-permute-done((bf16[424,256]{1,0:T(8,128)(2,1)S(1)}, bf16[424,256]{1,0:T(8,128)(2,1)S(1)}, u32[]{:S(2)}, u32[]{:S(2)}) %collective-permute-start.12) | collective-permute-done | bytes 217120 | tf_op jit(solution)/shard_map/ppermute | solution.py:26
  35.8 2.7 %collective-permute-start.17 = (bf16[424,256]{1,0:T(8,128)(2,1)S(1)}, bf16[424,256]{1,0:T(8,128)(2,1)S(1)}, u32[]{:S(2)}, u32[]{:S(2)}) collective-permute-start(bf16[424,256]{1,0:T(8,128)(2,1)S(1)} %collective-permute-done.16.rest_4_), channel_id=1, source_target_pairs={{0,7},{1,0},{2,1},{3,2},{4,3},{5,4},{6,5},{7,6},{8,15},{9,8},{10,9... | collective-permute-start | bytes 651272 | tf_op jit(solution)/shard_map/ppermute | solution.py:26
  38.4 1.9 %collective-permute-done.5.value_ref.rest_5_ = bf16[424,256]{1,0:T(8,128)(2,1)S(1)} collective-permute-done((bf16[424,256]{1,0:T(8,128)(2,1)S(1)}, bf16[424,256]{1,0:T(8,128)(2,1)S(1)}, u32[]{:S(2)}, u32[]{:S(2)}) %collective-permute-start.5) | collective-permute-done | bytes 217120 | tf_op jit(solution)/shard_map/ppermute | solution.py:26
  40.3 0.3 collective-permute-start.6
  40.6 2.7 %collective-permute-start.10 = (bf16[216,256]{1,0:T(8,128)(2,1)S(1)}, bf16[216,256]{1,0:T(8,128)(2,1)S(1)}, u32[]{:S(2)}, u32[]{:S(2)}) collective-permute-start(bf16[216,256]{1,0:T(8,128)(2,1)S(1)} %shard_map.70), channel_id=1, source_target_pairs={{0,7},{1,0},{2,1},{3,2},{4,3},{5,4},{6,5},{7,6},{8,15},{9,8},{10,9... | collective-permute-start | bytes 331784 | tf_op jit(solution)/shard_map/ppermute | solution.py:26
  43.3 0.8 convert_rsqrt_fusion
  44.1 0.2 broadcast_in_dim.5.scale_ref
  44.3 2.8 %convert.2.tile_0 = bf16[416,3392]{1,0:T(8,128)(2,1)S(1)} custom-call(s32[848,3392]{1,0:T(8,128)} %bitcast.6), custom_call_target="tpu_custom_call" | custom-call | flops 16777216 | bytes 9437184 | tf_op jit(solution)/shard_map/convert/pallas_call | solution.py:234
  47.1 2.9 %convert.3.tile_1 = bf16[432,3392]{1,0:T(8,128)(2,1)S(1)} custom-call(s32[848,3392]{1,0:T(8,128)} %bitcast.7), custom_call_target="tpu_custom_call" | custom-call | flops 16777216 | bytes 9437184 | tf_op jit(solution)/shard_map/convert/pallas_call | solution.py:234
  50.0 0.0 collective-permute-done.13.value_ref.rest_5_
  50.0 0.0 copy-start
  50.0 0.1 collective-permute-start.14
  50.1 0.0 collective-permute-done.17.value_ref.rest_6_
  50.1 2.7 %collective-permute-start.18 = (bf16[216,256]{1,0:T(8,128)(2,1)S(1)}, bf16[216,256]{1,0:T(8,128)(2,1)S(1)}, u32[]{:S(2)}, u32[]{:S(2)}) collective-permute-start(bf16[216,256]{1,0:T(8,128)(2,1)S(1)} %shard_map.74), channel_id=1, source_target_pairs={{0,7},{1,0},{2,1},{3,2},{4,3},{5,4},{6,5},{7,6},{8,15},{9,8},{10,9... | collective-permute-start | bytes 331784 | tf_op jit(solution)/shard_map/ppermute | solution.py:26
  52.9 0.2 shard_map.71
  53.1 0.2 shard_map.75
  53.3 0.0 collective-permute-done.6.rest_0_
  53.4 2.2 %shard_map.72 = (bf16[848,256]{1,0:T(8,128)(2,1)S(1)}, f32[256,512]{1,0:T(8,128)S(1)}, f32[3392,128]{1,0:T(8,128)S(1)}, f32[3392,128]{1,0:T(8,128)S(1)}) custom-call(s32[1]{0:T(128)} %bitcast.1.me_ref, bf16[416,3392]{1,0:T(8,128)(2,1)S(1)} %convert.2.tile_0, bf16[432,3392]{1,0:T(8,128)(2,1)S(1)} %convert.3.tile_1, ...), custom_call_target="tpu_custom_call", output_to_operand_aliasing={{2}: (7, {}), {3}: (8, {})} | custom-call | flops 1472724992 | bytes 1048576 | tf_op jit(solution)/shard_map/pallas_call | solution.py:30
  55.6 0.0 collective-permute-done.14.rest_0_
  55.6 0.0 copy-start.1
  55.6 2.3 %shard_map.76 = (bf16[848,256]{1,0:T(8,128)(2,1)S(1)}, f32[4,64,512]{2,1,0:T(8,128)S(1)}, bf16[4,64,512]{2,1,0:T(8,128)(2,1)S(1)}, f32[3392,128]{1,0:T(8,128)S(1)}, f32[3392,128]{1,0:T(8,128)S(1)}) custom-call(s32[1]{0:T(128)} %bitcast.1.me_ref, s32[1]{0:T(128)} %bitcast.2.core_ref.me_ref, ...), custom_call_target="tpu_custom_call", output_to_operand_aliasing={{3}: (9, {}), {4}: (10, {})} | custom-call | flops 1472724992 | bytes 1048576 | tf_op jit(solution)/shard_map/pallas_call | solution.py:30
  57.9 5.5 %collective-permute-start.19 = (bf16[4,64,512]{2,1,0:T(8,128)(2,1)S(1)}, bf16[4,64,512]{2,1,0:T(8,128)(2,1)S(1)}, u32[]{:S(2)}, u32[]{:S(2)}) collective-permute-start(bf16[4,64,512]{2,1,0:T(8,128)(2,1)S(1)} %get-tuple-element.47), channel_id=1, source_target_pairs={{0,32},{32,0},{64,96},{96,64},{128,160},{160,128},{192,224},{224,1... | collective-permute-start | bytes 786440 | tf_op jit(solution)/shard_map/ppermute | solution.py:194
  63.4 0.8 shard_map.79
  64.3 0.1 collective-permute-start.23
  64.4 0.2 collective-permute-done.19.got_ref
  64.6 0.1 shard_map.77
  64.7 1.4 %collective-permute-start.20 = (bf16[64,512]{1,0:T(8,128)(2,1)S(1)}, bf16[64,512]{1,0:T(8,128)(2,1)S(1)}, u32[]{:S(2)}, u32[]{:S(2)}) collective-permute-start(bf16[64,512]{1,0:T(8,128)(2,1)S(1)} %get-tuple-element.49), channel_id=1, source_target_pairs={{0,64},{32,96},{64,128},{96,160},{128,192},{160,224},{192,0},{224,... | collective-permute-start | bytes 196616 | tf_op jit(solution)/shard_map/ppermute | solution.py:200
  66.0 2.6 %collective-permute-start.21 = (bf16[64,512]{1,0:T(8,128)(2,1)S(1)}, bf16[64,512]{1,0:T(8,128)(2,1)S(1)}, u32[]{:S(2)}, u32[]{:S(2)}) collective-permute-start(bf16[64,512]{1,0:T(8,128)(2,1)S(1)} %get-tuple-element.50), channel_id=1, source_target_pairs={{0,128},{32,160},{64,192},{96,224},{128,0},{160,32},{192,64},{224,... | collective-permute-start | bytes 196616 | tf_op jit(solution)/shard_map/ppermute | solution.py:200
  68.7 1.1 %collective-permute-start.22 = (bf16[64,512]{1,0:T(8,128)(2,1)S(1)}, bf16[64,512]{1,0:T(8,128)(2,1)S(1)}, u32[]{:S(2)}, u32[]{:S(2)}) collective-permute-start(bf16[64,512]{1,0:T(8,128)(2,1)S(1)} %get-tuple-element.51), channel_id=1, source_target_pairs={{0,192},{32,224},{64,0},{96,32},{128,64},{160,96},{192,128},{224,1... | collective-permute-start | bytes 196616 | tf_op jit(solution)/shard_map/ppermute | solution.py:200
  69.7 1.8 %collective-permute-done.21.rest_1_ = bf16[64,512]{1,0:T(8,128)(2,1)S(1)} collective-permute-done((bf16[64,512]{1,0:T(8,128)(2,1)S(1)}, bf16[64,512]{1,0:T(8,128)(2,1)S(1)}, u32[]{:S(2)}, u32[]{:S(2)}) %collective-permute-start.21) | collective-permute-done | bytes 65568 | tf_op jit(solution)/shard_map/ppermute | solution.py:200
  71.6 0.5 collective-permute-done.22.rest_2_
  72.1 0.9 shard_map.78
  72.9 8.4 %all-to-all-start = ((f32[32,8,128]{2,1,0:T(8,128)}), f32[32,8,128]{2,1,0:T(8,128)S(1)}, u32[]{:S(2)}, u32[]{:S(2)}) async-start(f32[32,8,128]{2,1,0:T(8,128)} %shard_map.78), calls=%async_computation | async-start | bytes 262144 | tf_op jit(solution)/shard_map/all_to_all | solution.py:334
  81.3 0.1 shard_map.80
  81.4 0.1 collective-permute-start.24
  81.5 3.2 %collective-permute-start.25 = (bf16[64,848]{1,0:T(8,128)(2,1)S(1)}, bf16[64,848]{1,0:T(8,128)(2,1)S(1)}, u32[]{:S(2)}, u32[]{:S(2)}) collective-permute-start(bf16[64,848]{1,0:T(8,128)(2,1)S(1)} %get-tuple-element.58), channel_id=1, source_target_pairs={{0,128},{32,160},{64,192},{96,224},{128,0},{160,32},{192,64},{224,... | collective-permute-start | bytes 325640 | tf_op jit(solution)/shard_map/ppermute | solution.py:200
  84.7 0.4 collective-permute-start.26
  85.1 1.3 %collective-permute-done.24.rest_0_ = bf16[64,848]{1,0:T(8,128)(2,1)S(1)} collective-permute-done((bf16[64,848]{1,0:T(8,128)(2,1)S(1)}, bf16[64,848]{1,0:T(8,128)(2,1)S(1)}, u32[]{:S(2)}, u32[]{:S(2)}) %collective-permute-start.24) | collective-permute-done | bytes 108576 | tf_op jit(solution)/shard_map/ppermute | solution.py:200
  86.4 1.9 %collective-permute-done.25.rest_1_ = bf16[64,848]{1,0:T(8,128)(2,1)S(1)} collective-permute-done((bf16[64,848]{1,0:T(8,128)(2,1)S(1)}, bf16[64,848]{1,0:T(8,128)(2,1)S(1)}, u32[]{:S(2)}, u32[]{:S(2)}) %collective-permute-start.25) | collective-permute-done | bytes 108576 | tf_op jit(solution)/shard_map/ppermute | solution.py:200
  88.2 0.4 collective-permute-done.26.rest_2_
  88.6 1.8 %all-to-all-done.pieces_ref = f32[32,8,128]{2,1,0:T(8,128)S(1)} async-done(((f32[32,8,128]{2,1,0:T(8,128)}), f32[32,8,128]{2,1,0:T(8,128)S(1)}, u32[]{:S(2)}, u32[]{:S(2)}) %all-to-all-start) | async-done | bytes 131104 | tf_op jit(solution)/shard_map/all_to_all | solution.py:334
  90.5 0.8 shard_map.81
  (16 shorter events, 0.1 us)
Async XLA Ops:
  2.4 5.7 %collective-permute-start = (bf16[106,512]{1,0:T(8,128)(2,1)S(1)}, bf16[106,512]{1,0:T(8,128)(2,1)S(1)}, u32[]{:S(2)}, u32[]{:S(2)}) collective-permute-start(bf16[106,512]{1,0:T(8,128)(2,1)S(1)} %multiply_convert_fusion.refs_0_), channel_id=1, source_target_pairs={{0,8},{8,16},{16,24},{24,0},{1,9},{9,17},{17,25},{25,1},{2,10},{10... | collective-permute-start | bytes 325640 | tf_op jit(solution)/shard_map/ppermute | solution.py:26
  4.5 7.5 %collective-permute-start.1 = (bf16[106,512]{1,0:T(8,128)(2,1)S(1)}, bf16[106,512]{1,0:T(8,128)(2,1)S(1)}, u32[]{:S(2)}, u32[]{:S(2)}) collective-permute-start(bf16[106,512]{1,0:T(8,128)(2,1)S(1)} %multiply_convert_fusion.refs_0_), channel_id=1, source_target_pairs={{0,16},{8,24},{16,0},{24,8},{1,17},{9,25},{17,1},{25,9},{2,18},{10... | collective-permute-start | bytes 325640 | tf_op jit(solution)/shard_map/ppermute | solution.py:26
  7.0 5.0 %collective-permute-start.2 = (bf16[106,512]{1,0:T(8,128)(2,1)S(1)}, bf16[106,512]{1,0:T(8,128)(2,1)S(1)}, u32[]{:S(2)}, u32[]{:S(2)}) collective-permute-start(bf16[106,512]{1,0:T(8,128)(2,1)S(1)} %multiply_convert_fusion.refs_0_), channel_id=1, source_target_pairs={{0,24},{8,0},{16,8},{24,16},{1,25},{9,1},{17,9},{25,17},{2,26},{10... | collective-permute-start | bytes 325640 | tf_op jit(solution)/shard_map/ppermute | solution.py:26
  12.1 9.8 %collective-permute-start.3 = (bf16[424,256]{1,0:T(8,128)(2,1)S(1)}, bf16[424,256]{1,0:T(8,128)(2,1)S(1)}, u32[]{:S(2)}, u32[]{:S(2)}) collective-permute-start(bf16[424,256]{1,0:T(8,128)(2,1)S(1)} %get-tuple-element.39.rest_0_), channel_id=1, source_target_pairs={{0,1},{1,2},{2,3},{3,4},{4,5},{5,6},{6,7},{7,0},{8,9},{9,10},{10,1... | collective-permute-start | bytes 651272 | tf_op jit(solution)/shard_map/ppermute | solution.py:26
  13.8 8.1 %collective-permute-start.7 = (bf16[424,256]{1,0:T(8,128)(2,1)S(1)}, bf16[424,256]{1,0:T(8,128)(2,1)S(1)}, u32[]{:S(2)}, u32[]{:S(2)}) collective-permute-start(bf16[424,256]{1,0:T(8,128)(2,1)S(1)} %get-tuple-element.39.rest_0_), channel_id=1, source_target_pairs={{0,7},{1,0},{2,1},{3,2},{4,3},{5,4},{6,5},{7,6},{8,15},{9,8},{10,9... | collective-permute-start | bytes 651272 | tf_op jit(solution)/shard_map/ppermute | solution.py:26
  17.8 8.8 %collective-permute-start.11 = (bf16[424,256]{1,0:T(8,128)(2,1)S(1)}, bf16[424,256]{1,0:T(8,128)(2,1)S(1)}, u32[]{:S(2)}, u32[]{:S(2)}) collective-permute-start(bf16[424,256]{1,0:T(8,128)(2,1)S(1)} %get-tuple-element.43.rest_0_), channel_id=1, source_target_pairs={{0,1},{1,2},{2,3},{3,4},{4,5},{5,6},{6,7},{7,0},{8,9},{9,10},{10,1... | collective-permute-start | bytes 651272 | tf_op jit(solution)/shard_map/ppermute | solution.py:26
  17.8 8.8 %collective-permute-start.15 = (bf16[424,256]{1,0:T(8,128)(2,1)S(1)}, bf16[424,256]{1,0:T(8,128)(2,1)S(1)}, u32[]{:S(2)}, u32[]{:S(2)}) collective-permute-start(bf16[424,256]{1,0:T(8,128)(2,1)S(1)} %get-tuple-element.43.rest_0_), channel_id=1, source_target_pairs={{0,7},{1,0},{2,1},{3,2},{4,3},{5,4},{6,5},{7,6},{8,15},{9,8},{10,9... | collective-permute-start | bytes 651272 | tf_op jit(solution)/shard_map/ppermute | solution.py:26
  21.9 9.2 %collective-permute-start.4 = (bf16[424,256]{1,0:T(8,128)(2,1)S(1)}, bf16[424,256]{1,0:T(8,128)(2,1)S(1)}, u32[]{:S(2)}, u32[]{:S(2)}) collective-permute-start(bf16[424,256]{1,0:T(8,128)(2,1)S(1)} %collective-permute-done.3.rest_1_), channel_id=1, source_target_pairs={{0,1},{1,2},{2,3},{3,4},{4,5},{5,6},{6,7},{7,0},{8,9},{9,10},{10,1... | collective-permute-start | bytes 651272 | tf_op jit(solution)/shard_map/ppermute | solution.py:26
  21.9 9.2 %collective-permute-start.8 = (bf16[424,256]{1,0:T(8,128)(2,1)S(1)}, bf16[424,256]{1,0:T(8,128)(2,1)S(1)}, u32[]{:S(2)}, u32[]{:S(2)}) collective-permute-start(bf16[424,256]{1,0:T(8,128)(2,1)S(1)} %collective-permute-done.7.rest_2_), channel_id=1, source_target_pairs={{0,7},{1,0},{2,1},{3,2},{4,3},{5,4},{6,5},{7,6},{8,15},{9,8},{10,9... | collective-permute-start | bytes 651272 | tf_op jit(solution)/shard_map/ppermute | solution.py:26
  26.6 9.2 %collective-permute-start.12 = (bf16[424,256]{1,0:T(8,128)(2,1)S(1)}, bf16[424,256]{1,0:T(8,128)(2,1)S(1)}, u32[]{:S(2)}, u32[]{:S(2)}) collective-permute-start(bf16[424,256]{1,0:T(8,128)(2,1)S(1)} %collective-permute-done.11.rest_1_), channel_id=1, source_target_pairs={{0,1},{1,2},{2,3},{3,4},{4,5},{5,6},{6,7},{7,0},{8,9},{9,10},{10,1... | collective-permute-start | bytes 651272 | tf_op jit(solution)/shard_map/ppermute | solution.py:26
  26.6 9.2 %collective-permute-start.16 = (bf16[424,256]{1,0:T(8,128)(2,1)S(1)}, bf16[424,256]{1,0:T(8,128)(2,1)S(1)}, u32[]{:S(2)}, u32[]{:S(2)}) collective-permute-start(bf16[424,256]{1,0:T(8,128)(2,1)S(1)} %collective-permute-done.15.rest_2_), channel_id=1, source_target_pairs={{0,7},{1,0},{2,1},{3,2},{4,3},{5,4},{6,5},{7,6},{8,15},{9,8},{10,9... | collective-permute-start | bytes 651272 | tf_op jit(solution)/shard_map/ppermute | solution.py:26
  31.1 9.2 %collective-permute-start.5 = (bf16[424,256]{1,0:T(8,128)(2,1)S(1)}, bf16[424,256]{1,0:T(8,128)(2,1)S(1)}, u32[]{:S(2)}, u32[]{:S(2)}) collective-permute-start(bf16[424,256]{1,0:T(8,128)(2,1)S(1)} %collective-permute-done.4.rest_3_), channel_id=1, source_target_pairs={{0,1},{1,2},{2,3},{3,4},{4,5},{5,6},{6,7},{7,0},{8,9},{9,10},{10,1... | collective-permute-start | bytes 651272 | tf_op jit(solution)/shard_map/ppermute | solution.py:26
  31.1 9.5 %collective-permute-start.9 = (bf16[424,256]{1,0:T(8,128)(2,1)S(1)}, bf16[424,256]{1,0:T(8,128)(2,1)S(1)}, u32[]{:S(2)}, u32[]{:S(2)}) collective-permute-start(bf16[424,256]{1,0:T(8,128)(2,1)S(1)} %collective-permute-done.8.rest_4_), channel_id=1, source_target_pairs={{0,7},{1,0},{2,1},{3,2},{4,3},{5,4},{6,5},{7,6},{8,15},{9,8},{10,9... | collective-permute-start | bytes 651272 | tf_op jit(solution)/shard_map/ppermute | solution.py:26
  35.8 14.2 %collective-permute-start.13 = (bf16[424,256]{1,0:T(8,128)(2,1)S(1)}, bf16[424,256]{1,0:T(8,128)(2,1)S(1)}, u32[]{:S(2)}, u32[]{:S(2)}) collective-permute-start(bf16[424,256]{1,0:T(8,128)(2,1)S(1)} %collective-permute-done.12.rest_3_), channel_id=1, source_target_pairs={{0,1},{1,2},{2,3},{3,4},{4,5},{5,6},{6,7},{7,0},{8,9},{9,10},{10,1... | collective-permute-start | bytes 651272 | tf_op jit(solution)/shard_map/ppermute | solution.py:26
  35.8 14.4 %collective-permute-start.17 = (bf16[424,256]{1,0:T(8,128)(2,1)S(1)}, bf16[424,256]{1,0:T(8,128)(2,1)S(1)}, u32[]{:S(2)}, u32[]{:S(2)}) collective-permute-start(bf16[424,256]{1,0:T(8,128)(2,1)S(1)} %collective-permute-done.16.rest_4_), channel_id=1, source_target_pairs={{0,7},{1,0},{2,1},{3,2},{4,3},{5,4},{6,5},{7,6},{8,15},{9,8},{10,9... | collective-permute-start | bytes 651272 | tf_op jit(solution)/shard_map/ppermute | solution.py:26
  40.3 13.0 %collective-permute-start.6 = (bf16[208,256]{1,0:T(8,128)(2,1)S(1)}, bf16[208,256]{1,0:T(8,128)(2,1)S(1)}, u32[]{:S(2)}, u32[]{:S(2)}) collective-permute-start(bf16[208,256]{1,0:T(8,128)(2,1)S(1)} %shard_map.69), channel_id=1, source_target_pairs={{0,1},{1,2},{2,3},{3,4},{4,5},{5,6},{6,7},{7,0},{8,9},{9,10},{10,1... | collective-permute-start | bytes 319496 | tf_op jit(solution)/shard_map/ppermute | solution.py:26
  40.6 12.7 %collective-permute-start.10 = (bf16[216,256]{1,0:T(8,128)(2,1)S(1)}, bf16[216,256]{1,0:T(8,128)(2,1)S(1)}, u32[]{:S(2)}, u32[]{:S(2)}) collective-permute-start(bf16[216,256]{1,0:T(8,128)(2,1)S(1)} %shard_map.70), channel_id=1, source_target_pairs={{0,7},{1,0},{2,1},{3,2},{4,3},{5,4},{6,5},{7,6},{8,15},{9,8},{10,9... | collective-permute-start | bytes 331784 | tf_op jit(solution)/shard_map/ppermute | solution.py:26
  50.0 3.3 %copy-start = (bf16[848,512]{1,0:T(8,128)(2,1)S(1)}, bf16[848,512]{1,0:T(8,128)(2,1)}, u32[]{:S(2)}) copy-start(bf16[848,512]{1,0:T(8,128)(2,1)} %features_ref.3) | copy-start | bytes 2605060
  50.0 5.6 %collective-permute-start.14 = (bf16[208,256]{1,0:T(8,128)(2,1)S(1)}, bf16[208,256]{1,0:T(8,128)(2,1)S(1)}, u32[]{:S(2)}, u32[]{:S(2)}) collective-permute-start(bf16[208,256]{1,0:T(8,128)(2,1)S(1)} %shard_map.73), channel_id=1, source_target_pairs={{0,1},{1,2},{2,3},{3,4},{4,5},{5,6},{6,7},{7,0},{8,9},{9,10},{10,1... | collective-permute-start | bytes 319496 | tf_op jit(solution)/shard_map/ppermute | solution.py:26
  50.1 5.5 %collective-permute-start.18 = (bf16[216,256]{1,0:T(8,128)(2,1)S(1)}, bf16[216,256]{1,0:T(8,128)(2,1)S(1)}, u32[]{:S(2)}, u32[]{:S(2)}) collective-permute-start(bf16[216,256]{1,0:T(8,128)(2,1)S(1)} %shard_map.74), channel_id=1, source_target_pairs={{0,7},{1,0},{2,1},{3,2},{4,3},{5,4},{6,5},{7,6},{8,15},{9,8},{10,9... | collective-permute-start | bytes 331784 | tf_op jit(solution)/shard_map/ppermute | solution.py:26
  55.6 7.8 %copy-start.1 = (bf16[512,512]{1,0:T(8,128)(2,1)S(1)}, bf16[512,512]{1,0:T(8,128)(2,1)}, u32[]{:S(2)}) copy-start(bf16[512,512]{1,0:T(8,128)(2,1)} %weight_ref.1) | copy-start | bytes 1572868
  57.9 6.7 %collective-permute-start.19 = (bf16[4,64,512]{2,1,0:T(8,128)(2,1)S(1)}, bf16[4,64,512]{2,1,0:T(8,128)(2,1)S(1)}, u32[]{:S(2)}, u32[]{:S(2)}) collective-permute-start(bf16[4,64,512]{2,1,0:T(8,128)(2,1)S(1)} %get-tuple-element.47), channel_id=1, source_target_pairs={{0,32},{32,0},{64,96},{96,64},{128,160},{160,128},{192,224},{224,1... | collective-permute-start | bytes 786440 | tf_op jit(solution)/shard_map/ppermute | solution.py:194
  64.3 17.0 %collective-permute-start.23 = (bf16[4,64,848]{2,1,0:T(8,128)(2,1)S(1)}, bf16[4,64,848]{2,1,0:T(8,128)(2,1)S(1)}, u32[]{:S(2)}, u32[]{:S(2)}) collective-permute-start(bf16[4,64,848]{2,1,0:T(8,128)(2,1)S(1)} %get-tuple-element.55), channel_id=1, source_target_pairs={{0,32},{32,0},{64,96},{96,64},{128,160},{160,128},{192,224},{224,1... | collective-permute-start | bytes 1302536 | tf_op jit(solution)/shard_map/ppermute | solution.py:194
  64.7 5.1 %collective-permute-start.20 = (bf16[64,512]{1,0:T(8,128)(2,1)S(1)}, bf16[64,512]{1,0:T(8,128)(2,1)S(1)}, u32[]{:S(2)}, u32[]{:S(2)}) collective-permute-start(bf16[64,512]{1,0:T(8,128)(2,1)S(1)} %get-tuple-element.49), channel_id=1, source_target_pairs={{0,64},{32,96},{64,128},{96,160},{128,192},{160,224},{192,0},{224,... | collective-permute-start | bytes 196616 | tf_op jit(solution)/shard_map/ppermute | solution.py:200
  66.0 5.5 %collective-permute-start.21 = (bf16[64,512]{1,0:T(8,128)(2,1)S(1)}, bf16[64,512]{1,0:T(8,128)(2,1)S(1)}, u32[]{:S(2)}, u32[]{:S(2)}) collective-permute-start(bf16[64,512]{1,0:T(8,128)(2,1)S(1)} %get-tuple-element.50), channel_id=1, source_target_pairs={{0,128},{32,160},{64,192},{96,224},{128,0},{160,32},{192,64},{224,... | collective-permute-start | bytes 196616 | tf_op jit(solution)/shard_map/ppermute | solution.py:200
  68.7 3.4 %collective-permute-start.22 = (bf16[64,512]{1,0:T(8,128)(2,1)S(1)}, bf16[64,512]{1,0:T(8,128)(2,1)S(1)}, u32[]{:S(2)}, u32[]{:S(2)}) collective-permute-start(bf16[64,512]{1,0:T(8,128)(2,1)S(1)} %get-tuple-element.51), channel_id=1, source_target_pairs={{0,192},{32,224},{64,0},{96,32},{128,64},{160,96},{192,128},{224,1... | collective-permute-start | bytes 196616 | tf_op jit(solution)/shard_map/ppermute | solution.py:200
  72.9 17.6 %all-to-all-start = ((f32[32,8,128]{2,1,0:T(8,128)}), f32[32,8,128]{2,1,0:T(8,128)S(1)}, u32[]{:S(2)}, u32[]{:S(2)}) async-start(f32[32,8,128]{2,1,0:T(8,128)} %shard_map.78), calls=%async_computation | async-start | bytes 262144 | tf_op jit(solution)/shard_map/all_to_all | solution.py:334
  81.4 4.9 %collective-permute-start.24 = (bf16[64,848]{1,0:T(8,128)(2,1)S(1)}, bf16[64,848]{1,0:T(8,128)(2,1)S(1)}, u32[]{:S(2)}, u32[]{:S(2)}) collective-permute-start(bf16[64,848]{1,0:T(8,128)(2,1)S(1)} %get-tuple-element.57), channel_id=1, source_target_pairs={{0,64},{32,96},{64,128},{96,160},{128,192},{160,224},{192,0},{224,... | collective-permute-start | bytes 325640 | tf_op jit(solution)/shard_map/ppermute | solution.py:200
  81.5 6.7 %collective-permute-start.25 = (bf16[64,848]{1,0:T(8,128)(2,1)S(1)}, bf16[64,848]{1,0:T(8,128)(2,1)S(1)}, u32[]{:S(2)}, u32[]{:S(2)}) collective-permute-start(bf16[64,848]{1,0:T(8,128)(2,1)S(1)} %get-tuple-element.58), channel_id=1, source_target_pairs={{0,128},{32,160},{64,192},{96,224},{128,0},{160,32},{192,64},{224,... | collective-permute-start | bytes 325640 | tf_op jit(solution)/shard_map/ppermute | solution.py:200
  84.7 3.9 %collective-permute-start.26 = (bf16[64,848]{1,0:T(8,128)(2,1)S(1)}, bf16[64,848]{1,0:T(8,128)(2,1)S(1)}, u32[]{:S(2)}, u32[]{:S(2)}) collective-permute-start(bf16[64,848]{1,0:T(8,128)(2,1)S(1)} %get-tuple-element.59), channel_id=1, source_target_pairs={{0,192},{32,224},{64,0},{96,32},{128,64},{160,96},{192,128},{224,1... | collective-permute-start | bytes 325640 | tf_op jit(solution)/shard_map/ppermute | solution.py:200
